TPU v7x, 512 devices: a whole 4x4x16 slice. The times are simulated.
512 devices in a mesh: batch: 16 (over y, x), ctx: 32 (over z, core).
Axes of the slice: x: 4, y: 4, z: 16, core: 2. Of those that a mesh axis runs over, the one named last changes fastest.
Arguments:
- asked_for: bfloat16 [16, 4096, 64, 64], P('batch', 'ctx'), may hold values from -6 to 6
- offered: bfloat16 [16, 4096, 64, 64], P('batch', 'ctx'), may hold values from -6 to 6
- contents: bfloat16 [16, 4096, 64, 64], P('batch', 'ctx'), may hold values from -6 to 6
- out_weight: bfloat16 [4096, 4096], P('batch'), may hold values from -0.09375 to 0.09375
Outputs:
- layer_out: bfloat16 [16, 4096, 4096], P('batch', 'ctx')
All inputs are finite; a program needn't handle non-finite values.
Results may differ from a plain program's by a relative error of at most 0.006.
Values may be sent and summed in bfloat16 or wider, within the bound.
A program may use at most 128 MiB of HBM per device.

v0:
```python
import jax
import jax.numpy as jnp
from jax import lax
from jax.sharding import PartitionSpec as P


def packed_total(arrays, axis):
    ends = [0]
    for a in arrays:
        ends.append(ends[-1] + a.size)
    total = lax.psum(jnp.concatenate([a.ravel() for a in arrays]), axis)
    return tuple((total[b:e].reshape(a.shape) for a, b, e in zip(arrays, ends, ends[1:])))


def to_features(values):
    wide = values.astype(jnp.float32)
    return jax.nn.softplus(wide).astype(jnp.bfloat16)


def after_reading(read, count):
    result = read * count**0.5
    return result.astype(jnp.bfloat16)


def look_up(features, state, mass):
    top = jnp.einsum(
        "bthd,bhde->bthe", features, state.astype(jnp.bfloat16), preferred_element_type=jnp.float32
    )
    bottom = jnp.einsum("bthd,bhd->bth", features.astype(jnp.float32), mass)
    return top / (bottom + 0.001)[..., None]


def shards(asked_for, offered, contents, out_weight):
    query_feature, key_feature = (to_features(asked_for), to_features(offered))
    count = asked_for.shape[1] * lax.axis_size("ctx")
    part_state = jnp.einsum(
        "bthd,bthe->bhde", key_feature, contents, preferred_element_type=jnp.float32
    )
    part_mass = jnp.sum(key_feature.astype(jnp.float32), axis=1)
    state, mass = packed_total((part_state, part_mass), "ctx")
    read = look_up(query_feature, state / count, mass / count)
    mixed = after_reading(read, count)
    mixed = mixed.reshape(mixed.shape[0], mixed.shape[1], -1)
    return jnp.einsum(
        "btw,wv->btv",
        mixed,
        lax.all_gather(out_weight, "batch", axis=0, tiled=True),
        preferred_element_type=jnp.float32,
    ).astype(jnp.bfloat16)


def solution(mesh):
    in_specs = (
        P("batch", "ctx", None, None),
        P("batch", "ctx", None, None),
        P("batch", "ctx", None, None),
        P("batch", None),
    )
    out_specs = P("batch", "ctx", None)
    return jax.shard_map(shards, mesh=mesh, in_specs=in_specs, out_specs=out_specs, check_vma=False)
```

profile of v0, /device:TPU:1, one launch (start us, length us, event | category | flops | bytes accessed | tf_op | source)
XLA Modules:
  0.0 263.6 jit_solution(13410124035713011407)
XLA Ops:
  7.4 0.0 copy-start
  7.4 0.0 all-reduce.2.cloned.1.call-start
  7.4 2.6 convert_reduce_fusion
  10.0 0.0 copy-done
  10.0 3.9 %fusion.15 = f32[64,64,64]{2,1,0:T(8,128)} fusion(bf16[1,128,64,64]{1,3,2,0:T(8,128)(2,1)S(1)} %copy-done, bf16[1,128,64,64]{1,3,2,0:T(8,128)(2,1)} %param.5), kind=kOutput, calls=%fused_computation.26 | convolution fusion | flops 71303168 | bytes 3145728 | tf_op jit(solution)/shard_map/bthd,bthe->bhde/dot_general | solution.py:36
  13.8 1.8 reshape.70
  15.7 0.1 reshape.71
  15.7 1.1 pad_maximum_fusion
  16.8 0.0 all-reduce.2.cloned.1.call-update
  16.8 0.0 all-gather.2.cloned.1.call-start
  16.9 0.5 all-gather.2.cloned.1.call-update
  17.4 218.0 %all-reduce.2.cloned.1.call-done = f32[266240]{0:T(1024)} async-done(((f32[266240]{0:T(1024)}), f32[266240]{0:T(1024)}) %all-reduce.2.cloned.1.call-update) | async-done | bytes 1064976 | tf_op jit(solution)/shard_map/psum | solution.py:11
  235.4 1.3 fusion.14
  236.7 0.4 convert_element_type.38
  237.1 0.7 slice_multiply_fusion.1
  237.8 0.1 reshape.74
  237.9 0.0 copy-start.1
  237.9 2.6 fusion.19
  240.5 0.0 copy-done.1
  240.5 1.6 fusion.12
  242.1 0.0 all-gather.2.cloned.1.call-done
  242.1 14.0 %fusion = bf16[1,128,4096]{2,1,0:T(8,128)(2,1)} fusion(bf16[128,4096]{0,1:T(8,128)(2,1)S(1)} %bitcast.34, bf16[4096,4096]{1,0:T(8,128)(2,1)} %all-gather.2.cloned.1.call-done), kind=kOutput, calls=%fused_computation.3 | convolution fusion | flops 4295491584 | bytes 35651584 | tf_op jit(solution)/shard_map/btw,wv->btv/dot_general | solution.py:44
  (1 shorter events, 0.0 us)
Async XLA Ops:
  7.4 2.6 copy-start
  7.4 228.0 %all-reduce.2.cloned.1.call-start = ((), (), s32[]{:S(2)}) async-start(), calls=%async_computation | async-start | bytes 2129920 | tf_op jit(solution)/shard_map/psum | solution.py:11
  16.8 225.3 %all-gather.2.cloned.1.call-start = ((), (), s32[]{:S(2)}) async-start(), calls=%async_computation.1 | async-start | bytes 35651584 | tf_op jit(solution)/shard_map/all_gather | solution.py:47
  237.9 2.6 copy-start.1
Sparse Core Ops, SparseCore 0:
  17.0 218.3 all-reduce.1
Sparse Core Ops, SparseCore 1:
  20.3 217.2 all-gather.1
where the time goes:
time: 264 us
  waiting for transfers between devices  219 us (83%)
  matrix products  22.1 us (8%)
  between operations  14.9 us (6%)
  other arithmetic  5.7 us (2%)
    psum x1, waiting for transfers between devices, packed_total(): total = lax.psum(jnp.concatenate([a.ravel() for a in arrays]), axis)  218 us
    dot_general x1, matrix products, shards(): jnp.einsum('btw,wv->btv', mixed, lax.all_gather(out_weight, 'batch', axis...  14 us
  transfers between devices with their start and end apart: 2, of which 1 were waited for; matrix products, arithmetic and copies ran while one was open for 3% of the time, Pallas kernels for 0%

commit v1 on v0

v1 whole, which is shorter than its diff:
```python
import jax
import jax.numpy as jnp
from jax import lax
from jax.experimental import pallas as pl
from jax.experimental.pallas import tpu as pltpu
from jax.sharding import PartitionSpec as P

BF = jnp.bfloat16
F32 = jnp.float32
MESH = pl.DeviceIdType.MESH
D = 4096
T = 128
NC = 4
CW = 256
SR = 80
QP = 8


def feature(x):
    return jnp.log(1.0 + jnp.exp(x.astype(F32))).astype(BF)


def pack(s):
    m = s[64:72]
    hi = m.astype(BF).astype(F32)
    return jnp.concatenate([s[0:64], hi, m - hi], axis=0).astype(BF)


def unpack(b):
    f = b.astype(F32)
    m = f[64:72] + f[72:80]
    return jnp.concatenate([f[0:64], m, m], axis=0)


def kernel(
    q_hbm, k_hbm, v_hbm, w_hbm, out_ref,
    wbuf, qbuf, kbuf, vbuf, qf, st, dsend, drecv, r1s, r1r, acc, r2s, r2r, gat, mixed, obuf,
    lsem, w_ss, w_rs, q_ss, q_rs, d_ss, d_rs, r1_ss, r1_rs, r2_ss, r2_rs, g2_ss, g2_rs, g1_ss, g1_rs,
    gd_ss, gd_rs, o_ss, o_rs, semA, semB,
):
    b = lax.axis_index("batch")
    t = lax.axis_index("ctx")
    y, x = b // 4, b % 4
    z, core = t // 2, t % 2
    zp = z % 2
    me = 2 * zp + core
    sib = 2 * zp + (1 - core)
    zo = z + 1 - 2 * zp
    cls, m0 = z % 4, z // 4

    def dev(dy=0, dx=0, zz=None, cc=None):
        zz = z if zz is None else zz
        cc = core if cc is None else cc
        return (((y + dy) % 4) * 4 + (x + dx) % 4, zz * 2 + cc)

    def zdev(dz):
        return dev(zz=(z + dz + 16) % 16)

    lw = [
        pltpu.make_async_copy(
            w_hbm.at[:, pl.ds(pl.multiple_of(me * (NC * CW) + c * CW, CW), CW)],
            wbuf.at[c, pl.ds(pl.multiple_of(b * 256, 256), 256), :],
            lsem.at[c],
        )
        for c in range(NC)
    ]
    lk = pltpu.make_async_copy(k_hbm, kbuf, lsem.at[NC])
    lv = pltpu.make_async_copy(v_hbm, vbuf, lsem.at[NC + 1])
    lq = pltpu.make_async_copy(q_hbm, qbuf.at[me], lsem.at[NC + 2])
    for c in lw + [lk, lv, lq]:
        c.start()

    barrier = pltpu.get_barrier_semaphore()
    near = [
        dev(dx=1), dev(dx=3), dev(dy=1), dev(dy=3), dev(cc=1 - core),
        zdev(1), zdev(-1), zdev(2), zdev(-2), dev(zz=zo, cc=1 - core),
    ]
    for d in near:
        pl.semaphore_signal(barrier, inc=1, device_id=d, device_id_type=MESH)
    pl.semaphore_wait(barrier, len(near))
    for d in (zdev(2), zdev(-2)):
        pl.semaphore_signal(semA, inc=1, device_id=d, device_id_type=MESH)

    def wcopy(c, h, dy, dx, ty=0, tx=0):
        blk = ((y + dy) % 4) * 4 + (x + dx) % 4
        ref = wbuf.at[c, pl.ds(pl.multiple_of(blk * 256 + h * 128, 128), 128), :]
        return pltpu.make_async_remote_copy(
            src_ref=ref, dst_ref=ref, send_sem=w_ss,
            recv_sem=w_rs.at[c, h, ((dy - ty) % 4) * 4 + (dx - tx) % 4],
            device_id=dev(dy=ty % 4, dx=tx % 4), device_id_type=MESH,
        )

    def wd(h, dp, ds):
        return (ds % 4, dp % 4) if h == 0 else (dp % 4, ds % 4)

    def wsend(c, h, dp, ds, tp, ts):
        wcopy(c, h, *wd(h, dp, ds), *wd(h, tp, ts)).start()

    def wwait(c, h, dp, ds):
        wcopy(c, h, *wd(h, dp, ds)).wait_recv()

    def e0(c):
        for h in (0, 1):
            for tp, ts in ((1, 0), (-1, 0), (0, 1), (0, -1)):
                wsend(c, h, 0, 0, tp, ts)

    def e1(c):
        for h in (0, 1):
            wwait(c, h, -1, 0)
            if c % 2 == 0:
                wsend(c, h, -1, 0, 1, 0)
            wsend(c, h, -1, 0, 0, 1)
            wsend(c, h, -1, 0, 0, -1)
            wwait(c, h, 1, 0)
            if c % 2 == 1:
                wsend(c, h, 1, 0, -1, 0)
            wsend(c, h, 1, 0, 0, 1)
            wsend(c, h, 1, 0, 0, -1)

    def e3(c):
        for h in (0, 1):
            wwait(c, h, 2, 0)
            wsend(c, h, 2, 0, 0, 1)
            wsend(c, h, 2, 0, 0, -1)

    def e4(c):
        for h in (0, 1):
            for dp, ds in ((0, -1), (-1, 1), (1, -1), (2, 1)):
                wwait(c, h, dp, ds)
                wsend(c, h, dp, ds, 0, -ds)

    def e5(c):
        for h in (0, 1):
            for dp, ds in ((0, 1), (1, 1), (-1, -1), (2, -1), (0, 2), (1, 2), (-1, 2), (2, 2)):
                wwait(c, h, dp, ds)

    qr = D // QP

    def qcopy(slot, i, n, target, path):
        ref = qbuf.at[slot, pl.ds(i * qr, n * qr), :]
        return pltpu.make_async_remote_copy(
            src_ref=ref, dst_ref=ref, send_sem=q_ss, recv_sem=q_rs.at[path, i], device_id=target, device_id_type=MESH
        )

    zs = 2 * (1 - zp) + core
    zs2 = 2 * (1 - zp) + (1 - core)

    def qlink(lo, hi):
        for i in range(lo, hi):
            qcopy(me, i, 1, dev(zz=zo), 1).start()

    def qrelay(lo, hi):
        for i in range(lo, hi):
            qcopy(zs, i, 1, dev(zz=zo), 1).wait_recv()
            qcopy(zs, i, 1, dev(cc=1 - core), 2).start()

    def qfeat(slot, lo, hi):
        def body(i, _):
            r = pl.ds(pl.multiple_of(i * 128, 128), 128)
            qf[slot, r, :] = feature(qbuf[slot, r, :])
            return 0
        lax.fori_loop(lo * (32 // QP), hi * (32 // QP), body, 0)

    for c in range(NC):
        lw[c].wait()
        e0(c)
    lq.wait()
    qcopy(me, 0, QP, dev(cc=1 - core), 0).start()
    qlink(0, 2)

    lk.wait()
    lv.wait()
    lane = lax.broadcasted_iota(jnp.int32, (64, 128), 1) < 64
    ones = jnp.ones((16, 128), BF)
    nt = (((1,), (1,)), ((), ()))

    def partial(half, i):
        k, m = i // 4, i % 4
        r = pl.ds(pl.multiple_of((16 * half + 4 * m + k) * 128, 128), 128)
        kf = feature(kbuf[r, :])
        g = lax.dot_general(vbuf[r, :], kf, nt, preferred_element_type=F32)
        n = lax.dot_general(ones, kf, nt, preferred_element_type=F32)
        return k, m, jnp.concatenate([jnp.where(lane, g[0:64], g[64:128]), n], axis=0)

    def theirs(i, _):
        k, m, s = partial(1 - core, i)
        dsend[k, m] = pack(s)
        return 0

    def mine(i, _):
        k, m, s = partial(core, i)
        st[k, m] = s
        return 0

    lax.fori_loop(0, 16, theirs, 0)
    dcopy = pltpu.make_async_remote_copy(
        src_ref=dsend, dst_ref=drecv, send_sem=d_ss, recv_sem=d_rs, device_id=dev(cc=1 - core), device_id_type=MESH
    )
    dcopy.start()
    lax.fori_loop(0, 16, mine, 0)
    e1(0)
    dcopy.wait_recv()

    def chip_sum(i, _):
        k, m = i // 4, i % 4
        s = st[k, m] + unpack(drecv[k, m])
        st[k, m] = s
        r1s[k, m] = pack(s)
        return 0

    lax.fori_loop(0, 16, chip_sum, 0)

    def r1copy(n):
        dz, slot, lo, cnt = ((1, 0, 0, 4), (-1, 1, 0, 4), (2, 2, 0, 2), (-2, 2, 2, 2))[n]
        k = (z + dz + 16) % 4
        return pltpu.make_async_remote_copy(
            src_ref=r1s.at[k, pl.ds(lo, cnt)], dst_ref=r1r.at[slot, pl.ds(lo, cnt)],
            send_sem=r1_ss.at[n], recv_sem=r1_rs.at[n], device_id=zdev(dz), device_id_type=MESH,
        )

    for n in (2, 3, 0, 1):
        r1copy(n).start()
    qlink(2, 4)
    e1(1)
    pl.semaphore_wait(semA, 2)
    for d in (zdev(4), zdev(-4)):
        pl.semaphore_signal(semB, inc=1, device_id=d, device_id_type=MESH)
    qfeat(me, 0, QP)
    e1(2)
    for n in (0, 1, 2, 3):
        r1copy(n).wait_recv()

    def near_sum(m, _):
        s = st[cls, m] + unpack(r1r[0, m]) + unpack(r1r[1, m]) + unpack(r1r[2, m])
        acc[m] = s
        r2s[m] = pack(s)
        return 0

    lax.fori_loop(0, 4, near_sum, 0)

    def r2copy(r):
        return pltpu.make_async_remote_copy(
            src_ref=r2s.at[(m0 + r) % 4], dst_ref=r2r.at[r - 1],
            send_sem=r2_ss.at[r - 1], recv_sem=r2_rs.at[r - 1], device_id=zdev(4 * r), device_id_type=MESH,
        )

    pl.semaphore_wait(semB, 2)
    for r in (2, 1, 3):
        r2copy(r).start()
    qlink(4, 8)
    e1(3)
    qcopy(me, 0, QP, dev(cc=1 - core), 0).wait_recv()
    qfeat(sib, 0, QP)
    for c in range(NC):
        e3(c)
    qrelay(0, 4)
    for r in (1, 2, 3):
        r2copy(r).wait_recv()
    total = (acc[m0] + unpack(r2r[0]) + unpack(r2r[1]) + unpack(r2r[2])) * (1.0 / 4096.0)
    gat[core, cls, m0] = pack(total)

    def g2copy(r):
        ref = gat.at[core, cls, m0]
        return pltpu.make_async_remote_copy(
            src_ref=ref, dst_ref=ref, send_sem=g2_ss.at[r - 1], recv_sem=g2_rs.at[r - 1],
            device_id=zdev(4 * r), device_id_type=MESH,
        )

    for r in (2, 1, 3):
        g2copy(r).start()
    e4(0)
    qrelay(4, 8)
    qfeat(zs, 0, QP)
    e4(1)
    for r in (1, 2, 3):
        g2copy(r).wait_recv()

    def g1copy(n):
        dz, lo, cnt = ((1, 0, 4), (-1, 0, 4), (2, 0, 2), (-2, 2, 2))[n]
        ref = gat.at[core, cls, pl.ds(lo, cnt)]
        return pltpu.make_async_remote_copy(
            src_ref=ref, dst_ref=ref, send_sem=g1_ss.at[n], recv_sem=g1_rs.at[n],
            device_id=zdev(dz), device_id_type=MESH,
        )

    def gdcopy(dk):
        ref = gat.at[core, (cls + dk) % 4]
        return pltpu.make_async_remote_copy(
            src_ref=ref, dst_ref=ref, send_sem=gd_ss.at[dk], recv_sem=gd_rs.at[dk],
            device_id=dev(cc=1 - core), device_id_type=MESH,
        )

    for n in (2, 3, 0, 1):
        g1copy(n).start()
    gdcopy(0).start()
    e4(2)
    for i in range(QP):
        qcopy(zs2, i, 1, dev(cc=1 - core), 2).wait_recv()
    qfeat(zs2, 0, QP)
    g1copy(0).wait_recv()
    gdcopy(3).start()
    g1copy(1).wait_recv()
    gdcopy(1).start()
    g1copy(2).wait_recv()
    g1copy(3).wait_recv()
    gdcopy(2).start()
    e4(3)

    def mix(half, i):
        k, m = i // 4, i % 4
        pair = 16 * half + 4 * m + k
        r = pl.ds(pl.multiple_of(pair * 128, 128), 128)
        s = gat[half, k, m].astype(F32)
        a, n = s[0:64], s[64:80]
        lo16 = lane[0:16]
        lhs = jnp.concatenate(
            [jnp.where(lane, a, 0.0), jnp.where(lane, 0.0, a), jnp.where(lo16, n, 0.0), jnp.where(lo16, 0.0, n)], axis=0
        ).astype(BF)
        rhs = jnp.concatenate([qf[u, r, :] for u in range(4)], axis=1)
        g = jnp.dot(lhs, rhs, preferred_element_type=F32)
        r0 = 64.0 / (g[128:129] + g[136:137] + 1e-3)
        r1 = 64.0 / (g[144:145] + g[152:153] + 1e-3)
        got = jnp.concatenate([g[0:64] * r0, g[64:128] * r1], axis=0).astype(BF)
        mixed[:, r] = got.T

    lax.fori_loop(0, 16, lambda i, _: (mix(core, i), 0)[1], 0)
    for dk in range(4):
        gdcopy(dk).wait_recv()
    lax.fori_loop(0, 16, lambda i, _: (mix(1 - core, i), 0)[1], 0)

    def ocopy(c, r):
        s = (me + r) % 4
        return pltpu.make_async_remote_copy(
            src_ref=obuf.at[c, pl.ds(pl.multiple_of(s * T, T), T), :],
            dst_ref=out_ref.at[:, pl.ds(pl.multiple_of(me * (NC * CW) + c * CW, CW), CW)],
            send_sem=o_ss.at[c, r - 1], recv_sem=o_rs.at[c, r - 1],
            device_id=dev(zz=z - zp + s // 2, cc=s % 2), device_id_type=MESH,
        )

    for c in range(NC):
        e5(c)
        got = jnp.dot(mixed[...], wbuf[c], preferred_element_type=F32)
        obuf[c] = got.astype(BF)
        for r in (2, 1, 3):
            ocopy(c, r).start()
        out_ref[:, pl.ds(pl.multiple_of(me * (NC * CW) + c * CW, CW), CW)] = obuf[c, pl.ds(pl.multiple_of(me * T, T), T), :]

    for c in range(NC):
        for r in (1, 2, 3):
            ocopy(c, r).wait_recv()
    for c in range(NC):
        for r in (1, 2, 3):
            ocopy(c, r).wait_send()
    dcopy.wait_send()
    for n in range(4):
        r1copy(n).wait_send()
        g1copy(n).wait_send()
        gdcopy(n).wait_send()
    for r in (1, 2, 3):
        r2copy(r).wait_send()
        g2copy(r).wait_send()
    wref = wbuf.at[:, pl.ds(0, 3840), :]
    pltpu.make_async_copy(wref, wref, w_ss).wait()
    qref = qbuf.at[pl.ds(0, 3)]
    pltpu.make_async_copy(qref, qref, q_ss).wait()


def shards(asked_for, offered, contents, out_weight):
    def view(a):
        return jnp.transpose(a, (0, 2, 3, 1)).reshape(D, T)

    dma = pltpu.SemaphoreType.DMA
    hbm = pl.BlockSpec(memory_space=pl.ANY)
    out = pl.pallas_call(
        kernel,
        out_shape=jax.ShapeDtypeStruct((T, D), BF),
        in_specs=[hbm] * 4,
        out_specs=pl.BlockSpec(memory_space=pltpu.VMEM),
        scratch_shapes=[
            pltpu.VMEM((NC, D, CW), BF),
            pltpu.VMEM((4, D, T), BF),
            pltpu.VMEM((D, T), BF),
            pltpu.VMEM((D, T), BF),
            pltpu.VMEM((4, D, T), BF),
            pltpu.VMEM((4, 4, SR, 128), F32),
            pltpu.VMEM((4, 4, SR, 128), BF),
            pltpu.VMEM((4, 4, SR, 128), BF),
            pltpu.VMEM((4, 4, SR, 128), BF),
            pltpu.VMEM((3, 4, SR, 128), BF),
            pltpu.VMEM((4, SR, 128), F32),
            pltpu.VMEM((4, SR, 128), BF),
            pltpu.VMEM((3, SR, 128), BF),
            pltpu.VMEM((2, 4, 4, SR, 128), BF),
            pltpu.VMEM((4 * T, D), BF),
            pltpu.VMEM((NC, 4 * T, CW), BF),
            dma((NC + 3,)),
            dma, dma((NC, 2, 16)),
            dma, dma((3, QP)),
            dma, dma,
            dma((4,)), dma((4,)),
            dma((3,)), dma((3,)),
            dma((3,)), dma((3,)),
            dma((4,)), dma((4,)),
            dma((4,)), dma((4,)),
            dma((NC, 3)), dma((NC, 3)),
            pltpu.SemaphoreType.REGULAR, pltpu.SemaphoreType.REGULAR,
        ],
        compiler_params=pltpu.CompilerParams(
            collective_id=0, has_side_effects=True, vmem_limit_bytes=56 * 1024 * 1024
        ),
        name="attend_project",
    )(view(asked_for), view(offered), view(contents), out_weight)
    return out.reshape(1, T, D)


def solution(mesh):
    in_specs = (
        P("batch", "ctx", None, None),
        P("batch", "ctx", None, None),
        P("batch", "ctx", None, None),
        P("batch", None),
    )
    return jax.shard_map(shards, mesh=mesh, in_specs=in_specs, out_specs=P("batch", "ctx", None), check_vma=False)
```

time: 264 us -> 84.7 us (0.32)
  waiting for transfers between devices: 219 us -> 0 us
  Pallas kernels: 0 us -> 81.7 us
  matrix products: 22.1 us -> 0 us
  between operations: 14.9 us -> 0.01 us
  other arithmetic: 5.7 us -> 0 us
    psum x1 -> x0, waiting for transfers between devices: 218 us -> none  [packed_total(): total = lax.psum(jnp.concatenate([a.ravel() for a in arrays]), axis)]
    pallas_call x0 -> x1, Pallas kernels: none -> 81.7 us  [shards(): pl.pallas_call(kernel, out_shape=jax.ShapeDtypeStruct((T, D), BF), in_spe...]
    dot_general x4 -> x0, matrix products: 22.1 us -> none  [the longest x1 14 us: shards(): jnp.einsum('btw,wv->btv', mixed, lax.all_gather(out_weight, 'batch', axis...]
  transfers between devices with their start and end apart: 2 -> 0, of which waited for: 1 -> 0; matrix products, arithmetic and copies ran while one was open for 3% -> 0% of each run, Pallas kernels for 0% -> 0%
where the time goes in v1:
time: 84.7 us; the launch traced here: 84 us
  Pallas kernels  81.7 us (96%)
  local copies, waits for them, and re-layouts  2.29 us (3%)
    pallas_call x1, Pallas kernels, shards(): pl.pallas_call(kernel, out_shape=jax.ShapeDtypeStruct((T, D), BF), in_spe...  81.7 us
    unnamed x1, local copies, waits for them, and re-layouts  2.29 us

profile of v1, /device:TPU:1, one launch (start us, length us, event | category | flops | bytes accessed | tf_op | source)
XLA Modules:
  0.0 84.0 jit_solution(8085980394996263751)
XLA Ops:
  0.0 81.7 %attend_project.1 = bf16[128,4096]{1,0:T(8,128)(2,1)} custom-call(bf16[4096,128]{1,0:T(8,128)(2,1)} %bitcast.11, bf16[4096,128]{1,0:T(8,128)(2,1)} %bitcast.12, bf16[4096,128]{1,0:T(8,128)(2,1)} %bitcast.13, bf16[256,4096]{1,0:T(8,128)(2,1)} %w_hbm.1), custom_call_target="tpu_custom_call" | custom-call | tf_op jit(solution)/shard_map/attend_project/pallas_call | solution.py:374
  81.7 2.3 %copy.6 = bf16[1,128,4096]{2,1,0:T(8,128)(2,1)} copy(bf16[1,128,4096]{2,1,0:T(8,128)(2,1)} %bitcast.10) | data formatting | bytes 2097152

commit v2 on v1

--- a/solution.py
+++ b/solution.py
@@ -13,7 +13,7 @@
 NC = 4
 CW = 256
 SR = 80
-QP = 8
+QP = 16
 
 
 def feature(x):
@@ -34,7 +34,7 @@
 
 def kernel(
     q_hbm, k_hbm, v_hbm, w_hbm, out_ref,
-    wbuf, qbuf, kbuf, vbuf, qf, st, dsend, drecv, r1s, r1r, acc, r2s, r2r, gat, mixed, obuf,
+    wbuf, qbuf, kbuf, vbuf, qf, st, dsend, drecv, r1s, r1r, acc, r2s, r2r, gat, rhs, mixed, obuf,
     lsem, w_ss, w_rs, q_ss, q_rs, d_ss, d_rs, r1_ss, r1_rs, r2_ss, r2_rs, g2_ss, g2_rs, g1_ss, g1_rs,
     gd_ss, gd_rs, o_ss, o_rs, semA, semB,
 ):
@@ -157,58 +157,52 @@
     def qfeat(slot, lo, hi):
         def body(i, _):
             r = pl.ds(pl.multiple_of(i * 128, 128), 128)
-            qf[slot, r, :] = feature(qbuf[slot, r, :])
-            return 0
-        lax.fori_loop(lo * (32 // QP), hi * (32 // QP), body, 0)
-
-    for c in range(NC):
-        lw[c].wait()
-        e0(c)
-    lq.wait()
-    qcopy(me, 0, QP, dev(cc=1 - core), 0).start()
-    qlink(0, 2)
-
-    lk.wait()
-    lv.wait()
+            qf[pl.ds(pl.multiple_of(slot * T, T), T), r] = feature(qbuf[slot, r, :]).T
+            return 0
+        lax.fori_loop(lo * (32 // QP), hi * (32 // QP), body, 0, unroll=2)
+
+    def start():
+        for c in range(NC):
+            lw[c].wait()
+            e0(c)
+        lq.wait()
+        qcopy(me, 0, QP, dev(cc=1 - core), 0).start()
+        qlink(0, 3)
+
     lane = lax.broadcasted_iota(jnp.int32, (64, 128), 1) < 64
-    ones = jnp.ones((16, 128), BF)
     nt = (((1,), (1,)), ((), ()))
 
     def partial(half, i):
         k, m = i // 4, i % 4
         r = pl.ds(pl.multiple_of((16 * half + 4 * m + k) * 128, 128), 128)
         kf = feature(kbuf[r, :])
-        g = lax.dot_general(vbuf[r, :], kf, nt, preferred_element_type=F32)
-        n = lax.dot_general(ones, kf, nt, preferred_element_type=F32)
+        g = lax.dot_general(kf, vbuf[r, :], nt, preferred_element_type=F32)
+        n = lax.dot_general(jnp.ones((16, 128), BF), kf, nt, preferred_element_type=F32)
         return k, m, jnp.concatenate([jnp.where(lane, g[0:64], g[64:128]), n], axis=0)
 
-    def theirs(i, _):
-        k, m, s = partial(1 - core, i)
-        dsend[k, m] = pack(s)
-        return 0
-
-    def mine(i, _):
-        k, m, s = partial(core, i)
-        st[k, m] = s
-        return 0
-
-    lax.fori_loop(0, 16, theirs, 0)
     dcopy = pltpu.make_async_remote_copy(
         src_ref=dsend, dst_ref=drecv, send_sem=d_ss, recv_sem=d_rs, device_id=dev(cc=1 - core), device_id_type=MESH
     )
-    dcopy.start()
-    lax.fori_loop(0, 16, mine, 0)
-    e1(0)
-    dcopy.wait_recv()
-
-    def chip_sum(i, _):
-        k, m = i // 4, i % 4
-        s = st[k, m] + unpack(drecv[k, m])
-        st[k, m] = s
-        r1s[k, m] = pack(s)
-        return 0
-
-    lax.fori_loop(0, 16, chip_sum, 0)
+
+    def theirs():
+        lk.wait()
+        lv.wait()
+
+        def body(i, _):
+            k, m, s = partial(1 - core, i)
+            dsend[k, m] = pack(s)
+            return 0
+
+        lax.fori_loop(0, 16, body, 0, unroll=4)
+        dcopy.start()
+
+    def mine():
+        def body(i, _):
+            k, m, s = partial(core, i)
+            st[k, m] = s
+            return 0
+
+        lax.fori_loop(0, 16, body, 0, unroll=4)
 
     def r1copy(n):
         dz, slot, lo, cnt = ((1, 0, 0, 4), (-1, 1, 0, 4), (2, 2, 0, 2), (-2, 2, 2, 2))[n]
@@ -218,25 +212,24 @@
             send_sem=r1_ss.at[n], recv_sem=r1_rs.at[n], device_id=zdev(dz), device_id_type=MESH,
         )
 
-    for n in (2, 3, 0, 1):
-        r1copy(n).start()
-    qlink(2, 4)
-    e1(1)
-    pl.semaphore_wait(semA, 2)
-    for d in (zdev(4), zdev(-4)):
-        pl.semaphore_signal(semB, inc=1, device_id=d, device_id_type=MESH)
-    qfeat(me, 0, QP)
-    e1(2)
-    for n in (0, 1, 2, 3):
-        r1copy(n).wait_recv()
-
-    def near_sum(m, _):
-        s = st[cls, m] + unpack(r1r[0, m]) + unpack(r1r[1, m]) + unpack(r1r[2, m])
-        acc[m] = s
-        r2s[m] = pack(s)
-        return 0
-
-    lax.fori_loop(0, 4, near_sum, 0)
+    def chip_sum():
+        dcopy.wait_recv()
+
+        def body(i, _):
+            k, m = i // 4, i % 4
+            s = st[k, m] + unpack(drecv[k, m])
+            st[k, m] = s
+            r1s[k, m] = pack(s)
+            return 0
+
+        lax.fori_loop(0, 16, body, 0, unroll=4)
+        for n in (2, 3, 0, 1):
+            r1copy(n).start()
+
+    def far_ready():
+        pl.semaphore_wait(semA, 2)
+        for d in (zdev(4), zdev(-4)):
+            pl.semaphore_signal(semB, inc=1, device_id=d, device_id_type=MESH)
 
     def r2copy(r):
         return pltpu.make_async_remote_copy(
@@ -244,20 +237,20 @@
             send_sem=r2_ss.at[r - 1], recv_sem=r2_rs.at[r - 1], device_id=zdev(4 * r), device_id_type=MESH,
         )
 
-    pl.semaphore_wait(semB, 2)
-    for r in (2, 1, 3):
-        r2copy(r).start()
-    qlink(4, 8)
-    e1(3)
-    qcopy(me, 0, QP, dev(cc=1 - core), 0).wait_recv()
-    qfeat(sib, 0, QP)
-    for c in range(NC):
-        e3(c)
-    qrelay(0, 4)
-    for r in (1, 2, 3):
-        r2copy(r).wait_recv()
-    total = (acc[m0] + unpack(r2r[0]) + unpack(r2r[1]) + unpack(r2r[2])) * (1.0 / 4096.0)
-    gat[core, cls, m0] = pack(total)
+    def near_sum():
+        for n in (0, 1, 2, 3):
+            r1copy(n).wait_recv()
+
+        def body(m, _):
+            s = st[cls, m] + unpack(r1r[0, m]) + unpack(r1r[1, m]) + unpack(r1r[2, m])
+            acc[m] = s
+            r2s[m] = pack(s)
+            return 0
+
+        lax.fori_loop(0, 4, body, 0)
+        pl.semaphore_wait(semB, 2)
+        for r in (2, 1, 3):
+            r2copy(r).start()
 
     def g2copy(r):
         ref = gat.at[core, cls, m0]
@@ -266,14 +259,13 @@
             device_id=zdev(4 * r), device_id_type=MESH,
         )
 
-    for r in (2, 1, 3):
-        g2copy(r).start()
-    e4(0)
-    qrelay(4, 8)
-    qfeat(zs, 0, QP)
-    e4(1)
-    for r in (1, 2, 3):
-        g2copy(r).wait_recv()
+    def far_sum():
+        for r in (1, 2, 3):
+            r2copy(r).wait_recv()
+        total = (acc[m0] + unpack(r2r[0]) + unpack(r2r[1]) + unpack(r2r[2])) * (1.0 / (32 * T))
+        gat[core, cls, m0] = pack(total)
+        for r in (2, 1, 3):
+            g2copy(r).start()
 
     def g1copy(n):
         dz, lo, cnt = ((1, 0, 4), (-1, 0, 4), (2, 0, 2), (-2, 2, 2))[n]
@@ -290,43 +282,55 @@
             device_id=dev(cc=1 - core), device_id_type=MESH,
         )
 
-    for n in (2, 3, 0, 1):
-        g1copy(n).start()
-    gdcopy(0).start()
-    e4(2)
-    for i in range(QP):
-        qcopy(zs2, i, 1, dev(cc=1 - core), 2).wait_recv()
-    qfeat(zs2, 0, QP)
-    g1copy(0).wait_recv()
-    gdcopy(3).start()
-    g1copy(1).wait_recv()
-    gdcopy(1).start()
-    g1copy(2).wait_recv()
-    g1copy(3).wait_recv()
-    gdcopy(2).start()
-    e4(3)
-
-    def mix(half, i):
-        k, m = i // 4, i % 4
-        pair = 16 * half + 4 * m + k
-        r = pl.ds(pl.multiple_of(pair * 128, 128), 128)
-        s = gat[half, k, m].astype(F32)
-        a, n = s[0:64], s[64:80]
-        lo16 = lane[0:16]
-        lhs = jnp.concatenate(
-            [jnp.where(lane, a, 0.0), jnp.where(lane, 0.0, a), jnp.where(lo16, n, 0.0), jnp.where(lo16, 0.0, n)], axis=0
-        ).astype(BF)
-        rhs = jnp.concatenate([qf[u, r, :] for u in range(4)], axis=1)
-        g = jnp.dot(lhs, rhs, preferred_element_type=F32)
-        r0 = 64.0 / (g[128:129] + g[136:137] + 1e-3)
-        r1 = 64.0 / (g[144:145] + g[152:153] + 1e-3)
-        got = jnp.concatenate([g[0:64] * r0, g[64:128] * r1], axis=0).astype(BF)
-        mixed[:, r] = got.T
-
-    lax.fori_loop(0, 16, lambda i, _: (mix(core, i), 0)[1], 0)
-    for dk in range(4):
+    def far_back():
+        for r in (1, 2, 3):
+            g2copy(r).wait_recv()
+        for n in (2, 3, 0, 1):
+            g1copy(n).start()
+        gdcopy(0).start()
+        prep(core, cls)
+
+    def take(dk):
+        for n in {3: (0,), 1: (1,), 2: (2, 3)}[dk]:
+            g1copy(n).wait_recv()
+        gdcopy(dk).start()
+        prep(core, (cls + dk) % 4)
+
+    def twin(dk):
         gdcopy(dk).wait_recv()
-    lax.fori_loop(0, 16, lambda i, _: (mix(1 - core, i), 0)[1], 0)
+        prep(1 - core, (cls + dk) % 4)
+
+    def prep(half, k):
+        row = lax.broadcasted_iota(jnp.int32, (16, 256), 0)
+        col = lax.broadcasted_iota(jnp.int32, (16, 256), 1) // 128
+        pick = jnp.where(row == 8 * col, 1.0 / 64.0, 0.0).astype(BF)
+        zero = jnp.zeros((128, 128), BF)
+        for m in range(4):
+            s = gat[half, k, m]
+            a = s[0:64].astype(F32)
+            n = lax.dot_general(s[64:80], pick, (((0,), (0,)), ((), ())), preferred_element_type=F32)
+            pair = 16 * half + 4 * m + k
+            rhs[pair, 0:64, 0:128] = jnp.where(lane, a, 0.0).astype(BF)
+            rhs[pair, 64:128, 0:128] = jnp.where(lane, 0.0, a).astype(BF)
+            rhs[pair, 128:256, 0:128] = zero
+            rhs[pair, 0:64, 128:256] = jnp.where(lane, n[0:64, 0:128], 0.0).astype(BF)
+            rhs[pair, 64:128, 128:256] = jnp.where(lane, 0.0, n[64:128, 0:128]).astype(BF)
+            rhs[pair, 128:192, 128:256] = jnp.where(lane, n[0:64, 128:256], 0.0).astype(BF)
+            rhs[pair, 192:256, 128:256] = jnp.where(lane, 0.0, n[64:128, 128:256]).astype(BF)
+
+    def mix(lo, hi):
+        def body(i, _):
+            for j in range(4):
+                pair = 4 * i + j
+                r = pl.ds(pl.multiple_of(pair * 128, 128), 128)
+                w = rhs[pair]
+                for u in range(4):
+                    f = qf[u * T : (u + 1) * T, r]
+                    g = jnp.dot(jnp.concatenate([f, f], axis=1), w, preferred_element_type=F32)
+                    mixed[u * T : (u + 1) * T, r] = (g[:, 0:128] / (g[:, 128:256] + 1e-3 / 64.0)).astype(BF)
+            return 0
+
+        lax.fori_loop(lo // 4, hi // 4, body, 0)
 
     def ocopy(c, r):
         s = (me + r) % 4
@@ -337,32 +341,100 @@
             device_id=dev(zz=z - zp + s // 2, cc=s % 2), device_id_type=MESH,
         )
 
-    for c in range(NC):
-        e5(c)
-        got = jnp.dot(mixed[...], wbuf[c], preferred_element_type=F32)
-        obuf[c] = got.astype(BF)
+    def project(c):
+        for i in (0, 1):
+            rows = pl.ds(i * 2 * T, 2 * T)
+            obuf[c, rows] = jnp.dot(mixed[rows, :], wbuf[c], preferred_element_type=F32).astype(BF)
         for r in (2, 1, 3):
             ocopy(c, r).start()
         out_ref[:, pl.ds(pl.multiple_of(me * (NC * CW) + c * CW, CW), CW)] = obuf[c, pl.ds(pl.multiple_of(me * T, T), T), :]
 
-    for c in range(NC):
+    def qtwin(lo, hi):
+        for i in range(lo, hi):
+            qcopy(zs2, i, 1, dev(cc=1 - core), 2).wait_recv()
+
+    def o_wait():
+        for c in range(NC):
+            for r in (1, 2, 3):
+                ocopy(c, r).wait_recv()
+
+    def finish():
+        for c in range(NC):
+            for r in (1, 2, 3):
+                ocopy(c, r).wait_send()
+        dcopy.wait_send()
+        for n in range(4):
+            r1copy(n).wait_send()
+            g1copy(n).wait_send()
+            gdcopy(n).wait_send()
         for r in (1, 2, 3):
-            ocopy(c, r).wait_recv()
-    for c in range(NC):
-        for r in (1, 2, 3):
-            ocopy(c, r).wait_send()
-    dcopy.wait_send()
-    for n in range(4):
-        r1copy(n).wait_send()
-        g1copy(n).wait_send()
-        gdcopy(n).wait_send()
-    for r in (1, 2, 3):
-        r2copy(r).wait_send()
-        g2copy(r).wait_send()
-    wref = wbuf.at[:, pl.ds(0, 3840), :]
-    pltpu.make_async_copy(wref, wref, w_ss).wait()
-    qref = qbuf.at[pl.ds(0, 3)]
-    pltpu.make_async_copy(qref, qref, q_ss).wait()
+            r2copy(r).wait_send()
+            g2copy(r).wait_send()
+        wref = wbuf.at[:, pl.ds(0, 3840), :]
+        pltpu.make_async_copy(wref, wref, w_ss).wait()
+        qref = qbuf.at[pl.ds(0, 3)]
+        pltpu.make_async_copy(qref, qref, q_ss).wait()
+
+    plan = [
+        ("start", start),
+        ("theirs", theirs),
+        ("mine", mine),
+        ("chip_sum", chip_sum),
+        ("qlink1", lambda: qlink(3, 4)),
+        ("e1_0", lambda: e1(0)),
+        ("far_ready", far_ready),
+        ("e1_1", lambda: e1(1)),
+        ("near_sum", near_sum),
+        ("qlink2", lambda: qlink(4, 8)),
+        ("e1_2", lambda: e1(2)),
+        ("qf_me", lambda: qfeat(me, 0, QP)),
+        ("e1_3", lambda: e1(3)),
+        ("qsib", lambda: qcopy(me, 0, QP, dev(cc=1 - core), 0).wait_recv()),
+        ("qf_sib", lambda: qfeat(sib, 0, QP)),
+        ("e3_0", lambda: e3(0)),
+        ("far_sum", far_sum),
+        ("qlink3", lambda: qlink(8, 12)),
+        ("qrelay1", lambda: qrelay(0, 4)),
+        ("e3_1", lambda: e3(1)),
+        ("qf_zs", lambda: qfeat(zs, 0, 4)),
+        ("qrelay2", lambda: qrelay(4, 8)),
+        ("qf_zs2", lambda: qfeat(zs, 4, 8)),
+        ("qtwin1", lambda: qtwin(0, 8)),
+        ("qf_tw1", lambda: qfeat(zs2, 0, 8)),
+        ("e3_2", lambda: e3(2)),
+        ("far_back", far_back),
+        ("qlink4", lambda: qlink(12, QP)),
+        ("e3_3", lambda: e3(3)),
+        ("twin0", lambda: twin(0)),
+        ("e4_0", lambda: e4(0)),
+        ("take3", lambda: take(3)),
+        ("take1", lambda: take(1)),
+        ("twin3", lambda: twin(3)),
+        ("twin1", lambda: twin(1)),
+        ("take2", lambda: take(2)),
+        ("e4_1", lambda: e4(1)),
+        ("twin2", lambda: twin(2)),
+        ("mix0", lambda: mix(0, 16)),
+        ("e4_2", lambda: e4(2)),
+        ("qrelay3", lambda: qrelay(8, QP)),
+        ("qf_zs3", lambda: qfeat(zs, 8, QP)),
+        ("qtwin2", lambda: qtwin(8, QP)),
+        ("qf_tw2", lambda: qfeat(zs2, 8, QP)),
+        ("mix1", lambda: mix(16, 32)),
+        ("e5_0", lambda: e5(0)),
+        ("pr_0", lambda: project(0)),
+        ("e4_3", lambda: e4(3)),
+        ("e5_1", lambda: e5(1)),
+        ("pr_1", lambda: project(1)),
+        ("e5_2", lambda: e5(2)),
+        ("pr_2", lambda: project(2)),
+        ("e5_3", lambda: e5(3)),
+        ("pr_3", lambda: project(3)),
+        ("o_wait", o_wait),
+        ("finish", finish),
+    ]
+    for name, step in plan:
+        step()
 
 
 def shards(asked_for, offered, contents, out_weight):
@@ -381,7 +453,7 @@
             pltpu.VMEM((4, D, T), BF),
             pltpu.VMEM((D, T), BF),
             pltpu.VMEM((D, T), BF),
-            pltpu.VMEM((4, D, T), BF),
+            pltpu.VMEM((4 * T, D), BF),
             pltpu.VMEM((4, 4, SR, 128), F32),
             pltpu.VMEM((4, 4, SR, 128), BF),
             pltpu.VMEM((4, 4, SR, 128), BF),
@@ -391,6 +463,7 @@
             pltpu.VMEM((4, SR, 128), BF),
             pltpu.VMEM((3, SR, 128), BF),
             pltpu.VMEM((2, 4, 4, SR, 128), BF),
+            pltpu.VMEM((32, 256, 256), BF),
             pltpu.VMEM((4 * T, D), BF),
             pltpu.VMEM((NC, 4 * T, CW), BF),
             dma((NC + 3,)),

time: 84.7 us -> 75.8 us (0.89)
  Pallas kernels: 81.7 us -> 73.4 us
    pallas_call x1, Pallas kernels: 81.7 us -> 73.4 us  [shards(): pl.pallas_call(kernel, out_shape=jax.ShapeDtypeStruct((T, D), BF), in_spe...]
where the time goes in v2:
time: 75.8 us; the launch traced here: 75.7 us
  Pallas kernels  73.4 us (97%)
  local copies, waits for them, and re-layouts  2.29 us (3%)
    pallas_call x1, Pallas kernels, shards(): pl.pallas_call(kernel, out_shape=jax.ShapeDtypeStruct((T, D), BF), in_spe...  73.4 us
    unnamed x1, local copies, waits for them, and re-layouts  2.29 us

profile of v2, /device:TPU:1, one launch (start us, length us, event | category | flops | bytes accessed | tf_op | source)
XLA Modules:
  0.0 75.7 jit_solution(11093199134759526410)
XLA Ops:
  0.0 73.4 %attend_project.1 = bf16[128,4096]{1,0:T(8,128)(2,1)} custom-call(bf16[4096,128]{1,0:T(8,128)(2,1)} %bitcast.11, bf16[4096,128]{1,0:T(8,128)(2,1)} %bitcast.12, bf16[4096,128]{1,0:T(8,128)(2,1)} %bitcast.13, bf16[256,4096]{1,0:T(8,128)(2,1)} %w_hbm.1), custom_call_target="tpu_custom_call" | custom-call | tf_op jit(solution)/shard_map/attend_project/pallas_call | solution.py:446
  73.4 2.3 %copy.6 = bf16[1,128,4096]{2,1,0:T(8,128)(2,1)} copy(bf16[1,128,4096]{2,1,0:T(8,128)(2,1)} %bitcast.10) | data formatting | bytes 2097152

commit v3 on v2

--- a/solution.py
+++ b/solution.py
@@ -43,9 +43,10 @@
     y, x = b // 4, b % 4
     z, core = t // 2, t % 2
     zp = z % 2
-    me = 2 * zp + core
-    sib = 2 * zp + (1 - core)
-    zo = z + 1 - 2 * zp
+    quarter = 2 * zp + core
+    me, sib, zs, zs2 = core, 1 - core, 2 + core, 3 - core
+    znext = (z + 2 * core + 15) % 16
+    zback = (z - 2 * core + 17) % 16
     cls, m0 = z % 4, z // 4
 
     def dev(dy=0, dx=0, zz=None, cc=None):
@@ -58,7 +59,7 @@
 
     lw = [
         pltpu.make_async_copy(
-            w_hbm.at[:, pl.ds(pl.multiple_of(me * (NC * CW) + c * CW, CW), CW)],
+            w_hbm.at[:, pl.ds(pl.multiple_of(quarter * (NC * CW) + c * CW, CW), CW)],
             wbuf.at[c, pl.ds(pl.multiple_of(b * 256, 256), 256), :],
             lsem.at[c],
         )
@@ -73,7 +74,7 @@
     barrier = pltpu.get_barrier_semaphore()
     near = [
         dev(dx=1), dev(dx=3), dev(dy=1), dev(dy=3), dev(cc=1 - core),
-        zdev(1), zdev(-1), zdev(2), zdev(-2), dev(zz=zo, cc=1 - core),
+        zdev(1), zdev(-1), zdev(2), zdev(-2), dev(zz=znext, cc=1 - core),
     ]
     for d in near:
         pl.semaphore_signal(barrier, inc=1, device_id=d, device_id_type=MESH)
@@ -136,23 +137,21 @@
 
     qr = D // QP
 
-    def qcopy(slot, i, n, target, path):
-        ref = qbuf.at[slot, pl.ds(i * qr, n * qr), :]
-        return pltpu.make_async_remote_copy(
-            src_ref=ref, dst_ref=ref, send_sem=q_ss, recv_sem=q_rs.at[path, i], device_id=target, device_id_type=MESH
-        )
-
-    zs = 2 * (1 - zp) + core
-    zs2 = 2 * (1 - zp) + (1 - core)
+    def qcopy(slot, to, i, n, target, path):
+        r = pl.ds(i * qr, n * qr)
+        return pltpu.make_async_remote_copy(
+            src_ref=qbuf.at[slot, r, :], dst_ref=qbuf.at[to, r, :], send_sem=q_ss, recv_sem=q_rs.at[path, i],
+            device_id=target, device_id_type=MESH,
+        )
 
     def qlink(lo, hi):
         for i in range(lo, hi):
-            qcopy(me, i, 1, dev(zz=zo), 1).start()
+            qcopy(me, zs, i, 1, dev(zz=znext), 1).start()
 
     def qrelay(lo, hi):
         for i in range(lo, hi):
-            qcopy(zs, i, 1, dev(zz=zo), 1).wait_recv()
-            qcopy(zs, i, 1, dev(cc=1 - core), 2).start()
+            qcopy(zs, zs, i, 1, dev(cc=1 - core), 1).wait_recv()
+            qcopy(zs, zs, i, 1, dev(cc=1 - core), 2).start()
 
     def qfeat(slot, lo, hi):
         def body(i, _):
@@ -166,8 +165,8 @@
             lw[c].wait()
             e0(c)
         lq.wait()
-        qcopy(me, 0, QP, dev(cc=1 - core), 0).start()
-        qlink(0, 3)
+        qcopy(me, me, 0, QP, dev(cc=1 - core), 0).start()
+        qlink(0, 4)
 
     lane = lax.broadcasted_iota(jnp.int32, (64, 128), 1) < 64
     nt = (((1,), (1,)), ((), ()))
@@ -325,43 +324,66 @@
                 r = pl.ds(pl.multiple_of(pair * 128, 128), 128)
                 w = rhs[pair]
                 for u in range(4):
-                    f = qf[u * T : (u + 1) * T, r]
+                    t0 = pl.ds(u * T, T)
+                    f = qf[t0, r]
                     g = jnp.dot(jnp.concatenate([f, f], axis=1), w, preferred_element_type=F32)
-                    mixed[u * T : (u + 1) * T, r] = (g[:, 0:128] / (g[:, 128:256] + 1e-3 / 64.0)).astype(BF)
+                    mixed[t0, r] = (g[:, 0:128] / (g[:, 128:256] + 1e-3 / 64.0)).astype(BF)
             return 0
 
         lax.fori_loop(lo // 4, hi // 4, body, 0)
 
-    def ocopy(c, r):
-        s = (me + r) % 4
-        return pltpu.make_async_remote_copy(
-            src_ref=obuf.at[c, pl.ds(pl.multiple_of(s * T, T), T), :],
-            dst_ref=out_ref.at[:, pl.ds(pl.multiple_of(me * (NC * CW) + c * CW, CW), CW)],
-            send_sem=o_ss.at[c, r - 1], recv_sem=o_rs.at[c, r - 1],
-            device_id=dev(zz=z - zp + s // 2, cc=s % 2), device_id_type=MESH,
-        )
-
-    def project(c):
-        for i in (0, 1):
-            rows = pl.ds(i * 2 * T, 2 * T)
-            obuf[c, rows] = jnp.dot(mixed[rows, :], wbuf[c], preferred_element_type=F32).astype(BF)
-        for r in (2, 1, 3):
-            ocopy(c, r).start()
-        out_ref[:, pl.ds(pl.multiple_of(me * (NC * CW) + c * CW, CW), CW)] = obuf[c, pl.ds(pl.multiple_of(me * T, T), T), :]
+    others = ((sib, dev(cc=1 - core)), (zs, dev(zz=zback)), (zs2, dev(zz=znext, cc=1 - core)))
+
+    def rows(slot):
+        return pl.ds(pl.multiple_of(slot * T, T), T)
+
+    def cols(c):
+        return pl.ds(pl.multiple_of(quarter * (NC * CW) + c * CW, CW), CW)
+
+    def ocopy(c, n):
+        s, target = others[n]
+        return pltpu.make_async_remote_copy(
+            src_ref=obuf.at[c, rows(s), :], dst_ref=out_ref.at[:, cols(c)],
+            send_sem=o_ss.at[c, n], recv_sem=o_rs.at[c, n],
+            device_id=target, device_id_type=MESH,
+        )
+
+    def part(c, slot):
+        return jnp.dot(mixed[rows(slot), :], wbuf[c], preferred_element_type=F32).astype(BF)
+
+    def far_tokens(c):
+        obuf[c, rows(zs)] = part(c, zs)
+        obuf[c, rows(zs2)] = part(c, zs2)
+        ocopy(c, 1).start()
+        ocopy(c, 2).start()
+
+    def all_tokens(c):
+        far = pl.ds(2 * T, 2 * T)
+        obuf[c, far] = jnp.dot(mixed[far, :], wbuf[c], preferred_element_type=F32).astype(BF)
+        near = pl.ds(0, 2 * T)
+        obuf[c, near] = jnp.dot(mixed[near, :], wbuf[c], preferred_element_type=F32).astype(BF)
+        for n in (1, 2, 0):
+            ocopy(c, n).start()
+        out_ref[:, cols(c)] = obuf[c, rows(me)]
+
+    def near_tokens(c):
+        obuf[c, rows(sib)] = part(c, sib)
+        out_ref[:, cols(c)] = part(c, me)
+        ocopy(c, 0).start()
 
     def qtwin(lo, hi):
         for i in range(lo, hi):
-            qcopy(zs2, i, 1, dev(cc=1 - core), 2).wait_recv()
+            qcopy(zs2, zs2, i, 1, dev(cc=1 - core), 2).wait_recv()
 
     def o_wait():
         for c in range(NC):
-            for r in (1, 2, 3):
-                ocopy(c, r).wait_recv()
+            for n in (0, 1, 2):
+                ocopy(c, n).wait_recv()
 
     def finish():
         for c in range(NC):
-            for r in (1, 2, 3):
-                ocopy(c, r).wait_send()
+            for n in (0, 1, 2):
+                ocopy(c, n).wait_send()
         dcopy.wait_send()
         for n in range(4):
             r1copy(n).wait_send()
@@ -380,35 +402,36 @@
         ("theirs", theirs),
         ("mine", mine),
         ("chip_sum", chip_sum),
-        ("qlink1", lambda: qlink(3, 4)),
+        ("qlink1", lambda: qlink(4, 6)),
         ("e1_0", lambda: e1(0)),
         ("far_ready", far_ready),
+        ("near_sum", near_sum),
+        ("qlink2", lambda: qlink(6, 12)),
         ("e1_1", lambda: e1(1)),
-        ("near_sum", near_sum),
-        ("qlink2", lambda: qlink(4, 8)),
         ("e1_2", lambda: e1(2)),
         ("qf_me", lambda: qfeat(me, 0, QP)),
         ("e1_3", lambda: e1(3)),
-        ("qsib", lambda: qcopy(me, 0, QP, dev(cc=1 - core), 0).wait_recv()),
+        ("qsib", lambda: qcopy(sib, sib, 0, QP, dev(cc=1 - core), 0).wait_recv()),
         ("qf_sib", lambda: qfeat(sib, 0, QP)),
+        ("far_sum", far_sum),
+        ("qlink3", lambda: qlink(12, QP)),
         ("e3_0", lambda: e3(0)),
-        ("far_sum", far_sum),
-        ("qlink3", lambda: qlink(8, 12)),
-        ("qrelay1", lambda: qrelay(0, 4)),
+        ("qrelay1", lambda: qrelay(0, 8)),
+        ("qf_zs", lambda: qfeat(zs, 0, 8)),
         ("e3_1", lambda: e3(1)),
-        ("qf_zs", lambda: qfeat(zs, 0, 4)),
-        ("qrelay2", lambda: qrelay(4, 8)),
-        ("qf_zs2", lambda: qfeat(zs, 4, 8)),
         ("qtwin1", lambda: qtwin(0, 8)),
-        ("qf_tw1", lambda: qfeat(zs2, 0, 8)),
+        ("qf_tw", lambda: qfeat(zs2, 0, 8)),
+        ("far_back", far_back),
+        ("qrelay2", lambda: qrelay(8, QP)),
+        ("qf_zs2", lambda: qfeat(zs, 8, QP)),
         ("e3_2", lambda: e3(2)),
-        ("far_back", far_back),
-        ("qlink4", lambda: qlink(12, QP)),
+        ("twin0", lambda: twin(0)),
+        ("qtwin2", lambda: qtwin(8, QP)),
+        ("qf_tw2", lambda: qfeat(zs2, 8, QP)),
         ("e3_3", lambda: e3(3)),
-        ("twin0", lambda: twin(0)),
-        ("e4_0", lambda: e4(0)),
         ("take3", lambda: take(3)),
         ("take1", lambda: take(1)),
+        ("e4_0", lambda: e4(0)),
         ("twin3", lambda: twin(3)),
         ("twin1", lambda: twin(1)),
         ("take2", lambda: take(2)),
@@ -416,20 +439,17 @@
         ("twin2", lambda: twin(2)),
         ("mix0", lambda: mix(0, 16)),
         ("e4_2", lambda: e4(2)),
-        ("qrelay3", lambda: qrelay(8, QP)),
-        ("qf_zs3", lambda: qfeat(zs, 8, QP)),
-        ("qtwin2", lambda: qtwin(8, QP)),
-        ("qf_tw2", lambda: qfeat(zs2, 8, QP)),
         ("mix1", lambda: mix(16, 32)),
         ("e5_0", lambda: e5(0)),
-        ("pr_0", lambda: project(0)),
         ("e4_3", lambda: e4(3)),
+        ("pr_0", lambda: all_tokens(0)),
         ("e5_1", lambda: e5(1)),
-        ("pr_1", lambda: project(1)),
+        ("pr_1", lambda: all_tokens(1)),
         ("e5_2", lambda: e5(2)),
-        ("pr_2", lambda: project(2)),
+        ("pr_2", lambda: all_tokens(2)),
         ("e5_3", lambda: e5(3)),
-        ("pr_3", lambda: project(3)),
+        ("prf_3", lambda: far_tokens(3)),
+        ("prn_3", lambda: near_tokens(3)),
         ("o_wait", o_wait),
         ("finish", finish),
     ]
@@ -445,7 +465,7 @@
     hbm = pl.BlockSpec(memory_space=pl.ANY)
     out = pl.pallas_call(
         kernel,
-        out_shape=jax.ShapeDtypeStruct((T, D), BF),
+        out_shape=pltpu.VMEM((T, D), BF),
         in_specs=[hbm] * 4,
         out_specs=pl.BlockSpec(memory_space=pltpu.VMEM),
         scratch_shapes=[

time: 75.8 us -> 66.4 us (0.88)
  Pallas kernels: 73.4 us -> 65.3 us
  local copies, waits for them, and re-layouts: 2.29 us -> 0.97 us
    pallas_call x1, Pallas kernels: 73.4 us -> 65.3 us  [shards(): pl.pallas_call(kernel, out_shape=pltpu.VMEM((T, D), BF), in_specs=[hbm] *...]
    unnamed x1, local copies, waits for them, and re-layouts: 2.29 us -> 0.97 us
where the time goes in v3:
time: 66.4 us; the launch traced here: 66.3 us
  Pallas kernels  65.3 us (98%)
  local copies, waits for them, and re-layouts  0.97 us (1%)
    pallas_call x1, Pallas kernels, shards(): pl.pallas_call(kernel, out_shape=pltpu.VMEM((T, D), BF), in_specs=[hbm] *...  65.3 us

profile of v3, /device:TPU:1, one launch (start us, length us, event | category | flops | bytes accessed | tf_op | source)
XLA Modules:
  0.0 66.3 jit_solution(15914222393587188268)
XLA Ops:
  0.0 65.3 %attend_project.1 = bf16[128,4096]{1,0:T(8,128)(2,1)S(1)} custom-call(bf16[4096,128]{1,0:T(8,128)(2,1)} %bitcast.11, bf16[4096,128]{1,0:T(8,128)(2,1)} %bitcast.12, bf16[4096,128]{1,0:T(8,128)(2,1)} %bitcast.13, bf16[256,4096]{1,0:T(8,128)(2,1)} %w_hbm.1), custom_call_target="tpu_custom_call" | custom-call | tf_op jit(solution)/shard_map/attend_project/pallas_call | solution.py:466
  65.3 1.0 %copy.6 = bf16[1,128,4096]{2,1,0:T(8,128)(2,1)} copy(bf16[1,128,4096]{2,1,0:T(8,128)(2,1)S(1)} %bitcast.10) | data formatting | bytes 2097152

commit v4 on v3

--- a/solution.py
+++ b/solution.py
@@ -35,8 +35,7 @@
 def kernel(
     q_hbm, k_hbm, v_hbm, w_hbm, out_ref,
     wbuf, qbuf, kbuf, vbuf, qf, st, dsend, drecv, r1s, r1r, acc, r2s, r2r, gat, rhs, mixed, obuf,
-    lsem, w_ss, w_rs, q_ss, q_rs, d_ss, d_rs, r1_ss, r1_rs, r2_ss, r2_rs, g2_ss, g2_rs, g1_ss, g1_rs,
-    gd_ss, gd_rs, o_ss, o_rs, semA, semB,
+    lsem, w_ss, w_rs, q_ss, q_rs, s_ss, d_rs, r1_rs, r2_rs, g2_rs, g1_rs, gd_rs, o_ss, o_rs, semA, semB, semP, semZ,
 ):
     b = lax.axis_index("batch")
     t = lax.axis_index("ctx")
@@ -72,33 +71,60 @@
         c.start()
 
     barrier = pltpu.get_barrier_semaphore()
-    near = [
-        dev(dx=1), dev(dx=3), dev(dy=1), dev(dy=3), dev(cc=1 - core),
-        zdev(1), zdev(-1), zdev(2), zdev(-2), dev(zz=znext, cc=1 - core),
-    ]
-    for d in near:
-        pl.semaphore_signal(barrier, inc=1, device_id=d, device_id_type=MESH)
-    pl.semaphore_wait(barrier, len(near))
-    for d in (zdev(2), zdev(-2)):
-        pl.semaphore_signal(semA, inc=1, device_id=d, device_id_type=MESH)
-
-    def wcopy(c, h, dy, dx, ty=0, tx=0):
-        blk = ((y + dy) % 4) * 4 + (x + dx) % 4
+
+    def tell(sem, d):
+        pl.semaphore_signal(sem, inc=1, device_id=d, device_id_type=MESH)
+
+    twin_core = dev(cc=1 - core)
+    for dy, dx in ((0, 1), (0, 3), (1, 0), (3, 0)):
+        tell(barrier, dev(dy=dy, dx=dx, cc=0))
+    for dz in (1, -1, 2, -2):
+        tell(barrier, dev(zz=(z + dz + 16) % 16, cc=1))
+
+    @pl.when(core == 1)
+    def _():
+        tell(barrier, twin_core)
+
+    @pl.when(core == 0)
+    def _():
+        pl.semaphore_wait(barrier, 9)
+        tell(semP, twin_core)
+
+    @pl.when(core == 1)
+    def _():
+        pl.semaphore_wait(semP, 1)
+
+    def z_ready():
+        @pl.when(core == 1)
+        def _():
+            pl.semaphore_wait(barrier, 8)
+            tell(semZ, twin_core)
+
+        @pl.when(core == 0)
+        def _():
+            pl.semaphore_wait(semZ, 1)
+
+        for d in (zdev(2), zdev(-2)):
+            tell(semA, d)
+
+    def drain(ref, sem):
+        pltpu.make_async_copy(ref, ref, sem).wait()
+
+    groups = {(1, 0): 0, (3, 0): 0, (2, 0): 1, (0, 3): 2, (3, 1): 2, (1, 3): 3, (2, 1): 3}
+
+    def wsend(c, h, dp, ds, tp, ts):
+        dy, dx = (ds, dp) if h == 0 else (dp, ds)
+        ty, tx = (ts, tp) if h == 0 else (tp, ts)
+        blk = ((y + dy + 4) % 4) * 4 + (x + dx + 4) % 4
         ref = wbuf.at[c, pl.ds(pl.multiple_of(blk * 256 + h * 128, 128), 128), :]
-        return pltpu.make_async_remote_copy(
+        pltpu.make_async_remote_copy(
             src_ref=ref, dst_ref=ref, send_sem=w_ss,
-            recv_sem=w_rs.at[c, h, ((dy - ty) % 4) * 4 + (dx - tx) % 4],
+            recv_sem=w_rs.at[c, groups.get(((dp - tp) % 4, (ds - ts) % 4), 4)],
             device_id=dev(dy=ty % 4, dx=tx % 4), device_id_type=MESH,
-        )
-
-    def wd(h, dp, ds):
-        return (ds % 4, dp % 4) if h == 0 else (dp % 4, ds % 4)
-
-    def wsend(c, h, dp, ds, tp, ts):
-        wcopy(c, h, *wd(h, dp, ds), *wd(h, tp, ts)).start()
-
-    def wwait(c, h, dp, ds):
-        wcopy(c, h, *wd(h, dp, ds)).wait_recv()
+        ).start()
+
+    def wwait(c, g):
+        drain(wbuf.at[c, pl.ds(0, (4, 2, 4, 4, 16)[g] * 128), :], w_rs.at[c, g])
 
     def e0(c):
         for h in (0, 1):
@@ -106,52 +132,47 @@
                 wsend(c, h, 0, 0, tp, ts)
 
     def e1(c):
+        wwait(c, 0)
         for h in (0, 1):
-            wwait(c, h, -1, 0)
-            if c % 2 == 0:
-                wsend(c, h, -1, 0, 1, 0)
-            wsend(c, h, -1, 0, 0, 1)
-            wsend(c, h, -1, 0, 0, -1)
-            wwait(c, h, 1, 0)
-            if c % 2 == 1:
-                wsend(c, h, 1, 0, -1, 0)
-            wsend(c, h, 1, 0, 0, 1)
-            wsend(c, h, 1, 0, 0, -1)
+            wsend(c, h, *(((-1, 0, 1, 0), (1, 0, -1, 0))[c % 2]))
+            for dp in (-1, 1):
+                wsend(c, h, dp, 0, 0, 1)
+                wsend(c, h, dp, 0, 0, -1)
 
     def e3(c):
+        wwait(c, 1)
         for h in (0, 1):
-            wwait(c, h, 2, 0)
             wsend(c, h, 2, 0, 0, 1)
             wsend(c, h, 2, 0, 0, -1)
 
-    def e4(c):
+    def e4(c, late):
+        wwait(c, 2 + late)
         for h in (0, 1):
-            for dp, ds in ((0, -1), (-1, 1), (1, -1), (2, 1)):
-                wwait(c, h, dp, ds)
+            for dp, ds in (((0, -1), (-1, 1)), ((1, -1), (2, 1)))[late]:
                 wsend(c, h, dp, ds, 0, -ds)
 
     def e5(c):
-        for h in (0, 1):
-            for dp, ds in ((0, 1), (1, 1), (-1, -1), (2, -1), (0, 2), (1, 2), (-1, 2), (2, 2)):
-                wwait(c, h, dp, ds)
+        wwait(c, 4)
 
     qr = D // QP
 
-    def qcopy(slot, to, i, n, target, path):
+    def qcopy(slot, to, i, n, target, sem):
         r = pl.ds(i * qr, n * qr)
-        return pltpu.make_async_remote_copy(
-            src_ref=qbuf.at[slot, r, :], dst_ref=qbuf.at[to, r, :], send_sem=q_ss, recv_sem=q_rs.at[path, i],
+        pltpu.make_async_remote_copy(
+            src_ref=qbuf.at[slot, r, :], dst_ref=qbuf.at[to, r, :], send_sem=q_ss, recv_sem=q_rs.at[sem],
             device_id=target, device_id_type=MESH,
-        )
+        ).start()
+
+    def qwait(sem, n):
+        drain(qbuf.at[0, pl.ds(0, n * qr), :], q_rs.at[sem])
 
     def qlink(lo, hi):
         for i in range(lo, hi):
-            qcopy(me, zs, i, 1, dev(zz=znext), 1).start()
-
-    def qrelay(lo, hi):
-        for i in range(lo, hi):
-            qcopy(zs, zs, i, 1, dev(cc=1 - core), 1).wait_recv()
-            qcopy(zs, zs, i, 1, dev(cc=1 - core), 2).start()
+            qcopy(me, zs, i, 1, dev(zz=znext), 1 + i // 8)
+
+    def qrelay(half):
+        qwait(1 + half, 8)
+        qcopy(zs, zs, 8 * half, 8, twin_core, 3 + half)
 
     def qfeat(slot, lo, hi):
         def body(i, _):
@@ -165,8 +186,7 @@
             lw[c].wait()
             e0(c)
         lq.wait()
-        qcopy(me, me, 0, QP, dev(cc=1 - core), 0).start()
-        qlink(0, 4)
+        qcopy(me, me, 0, QP, twin_core, 0)
 
     lane = lax.broadcasted_iota(jnp.int32, (64, 128), 1) < 64
     nt = (((1,), (1,)), ((), ()))
@@ -180,7 +200,7 @@
         return k, m, jnp.concatenate([jnp.where(lane, g[0:64], g[64:128]), n], axis=0)
 
     dcopy = pltpu.make_async_remote_copy(
-        src_ref=dsend, dst_ref=drecv, send_sem=d_ss, recv_sem=d_rs, device_id=dev(cc=1 - core), device_id_type=MESH
+        src_ref=dsend, dst_ref=drecv, send_sem=s_ss, recv_sem=d_rs, device_id=dev(cc=1 - core), device_id_type=MESH
     )
 
     def theirs():
@@ -208,7 +228,7 @@
         k = (z + dz + 16) % 4
         return pltpu.make_async_remote_copy(
             src_ref=r1s.at[k, pl.ds(lo, cnt)], dst_ref=r1r.at[slot, pl.ds(lo, cnt)],
-            send_sem=r1_ss.at[n], recv_sem=r1_rs.at[n], device_id=zdev(dz), device_id_type=MESH,
+            send_sem=s_ss, recv_sem=r1_rs, device_id=zdev(dz), device_id_type=MESH,
         )
 
     def chip_sum():
@@ -233,12 +253,11 @@
     def r2copy(r):
         return pltpu.make_async_remote_copy(
             src_ref=r2s.at[(m0 + r) % 4], dst_ref=r2r.at[r - 1],
-            send_sem=r2_ss.at[r - 1], recv_sem=r2_rs.at[r - 1], device_id=zdev(4 * r), device_id_type=MESH,
+            send_sem=s_ss, recv_sem=r2_rs, device_id=zdev(4 * r), device_id_type=MESH,
         )
 
     def near_sum():
-        for n in (0, 1, 2, 3):
-            r1copy(n).wait_recv()
+        drain(r1r, r1_rs)
 
         def body(m, _):
             s = st[cls, m] + unpack(r1r[0, m]) + unpack(r1r[1, m]) + unpack(r1r[2, m])
@@ -254,13 +273,12 @@
     def g2copy(r):
         ref = gat.at[core, cls, m0]
         return pltpu.make_async_remote_copy(
-            src_ref=ref, dst_ref=ref, send_sem=g2_ss.at[r - 1], recv_sem=g2_rs.at[r - 1],
+            src_ref=ref, dst_ref=ref, send_sem=s_ss, recv_sem=g2_rs,
             device_id=zdev(4 * r), device_id_type=MESH,
         )
 
     def far_sum():
-        for r in (1, 2, 3):
-            r2copy(r).wait_recv()
+        drain(r2r, r2_rs)
         total = (acc[m0] + unpack(r2r[0]) + unpack(r2r[1]) + unpack(r2r[2])) * (1.0 / (32 * T))
         gat[core, cls, m0] = pack(total)
         for r in (2, 1, 3):
@@ -270,28 +288,26 @@
         dz, lo, cnt = ((1, 0, 4), (-1, 0, 4), (2, 0, 2), (-2, 2, 2))[n]
         ref = gat.at[core, cls, pl.ds(lo, cnt)]
         return pltpu.make_async_remote_copy(
-            src_ref=ref, dst_ref=ref, send_sem=g1_ss.at[n], recv_sem=g1_rs.at[n],
+            src_ref=ref, dst_ref=ref, send_sem=s_ss, recv_sem=g1_rs.at[min(n, 2)],
             device_id=zdev(dz), device_id_type=MESH,
         )
 
     def gdcopy(dk):
         ref = gat.at[core, (cls + dk) % 4]
         return pltpu.make_async_remote_copy(
-            src_ref=ref, dst_ref=ref, send_sem=gd_ss.at[dk], recv_sem=gd_rs.at[dk],
+            src_ref=ref, dst_ref=ref, send_sem=s_ss, recv_sem=gd_rs.at[dk],
             device_id=dev(cc=1 - core), device_id_type=MESH,
         )
 
     def far_back():
-        for r in (1, 2, 3):
-            g2copy(r).wait_recv()
+        drain(r2r, g2_rs)
         for n in (2, 3, 0, 1):
             g1copy(n).start()
         gdcopy(0).start()
         prep(core, cls)
 
     def take(dk):
-        for n in {3: (0,), 1: (1,), 2: (2, 3)}[dk]:
-            g1copy(n).wait_recv()
+        drain(gat.at[core, cls], g1_rs.at[{3: 0, 1: 1, 2: 2}[dk]])
         gdcopy(dk).start()
         prep(core, (cls + dk) % 4)
 
@@ -344,7 +360,7 @@
         s, target = others[n]
         return pltpu.make_async_remote_copy(
             src_ref=obuf.at[c, rows(s), :], dst_ref=out_ref.at[:, cols(c)],
-            send_sem=o_ss.at[c, n], recv_sem=o_rs.at[c, n],
+            send_sem=o_ss, recv_sem=o_rs,
             device_id=target, device_id_type=MESH,
         )
 
@@ -371,38 +387,23 @@
         out_ref[:, cols(c)] = part(c, me)
         ocopy(c, 0).start()
 
-    def qtwin(lo, hi):
-        for i in range(lo, hi):
-            qcopy(zs2, zs2, i, 1, dev(cc=1 - core), 2).wait_recv()
-
     def o_wait():
-        for c in range(NC):
-            for n in (0, 1, 2):
-                ocopy(c, n).wait_recv()
+        drain(obuf.at[pl.ds(0, 3)], o_rs)
 
     def finish():
-        for c in range(NC):
-            for n in (0, 1, 2):
-                ocopy(c, n).wait_send()
-        dcopy.wait_send()
-        for n in range(4):
-            r1copy(n).wait_send()
-            g1copy(n).wait_send()
-            gdcopy(n).wait_send()
-        for r in (1, 2, 3):
-            r2copy(r).wait_send()
-            g2copy(r).wait_send()
-        wref = wbuf.at[:, pl.ds(0, 3840), :]
-        pltpu.make_async_copy(wref, wref, w_ss).wait()
-        qref = qbuf.at[pl.ds(0, 3)]
-        pltpu.make_async_copy(qref, qref, q_ss).wait()
+        drain(obuf.at[pl.ds(0, 3)], o_ss)
+        drain(wbuf.at[0, pl.ds(0, 2480), :], s_ss)
+        drain(wbuf.at[:, pl.ds(0, 3840), :], w_ss)
+        drain(qbuf.at[pl.ds(0, 3)], q_ss)
 
     plan = [
         ("start", start),
         ("theirs", theirs),
         ("mine", mine),
+        ("z_ready", z_ready),
+        ("qlink0", lambda: qlink(0, 2)),
         ("chip_sum", chip_sum),
-        ("qlink1", lambda: qlink(4, 6)),
+        ("qlink1", lambda: qlink(2, 6)),
         ("e1_0", lambda: e1(0)),
         ("far_ready", far_ready),
         ("near_sum", near_sum),
@@ -411,37 +412,41 @@
         ("e1_2", lambda: e1(2)),
         ("qf_me", lambda: qfeat(me, 0, QP)),
         ("e1_3", lambda: e1(3)),
-        ("qsib", lambda: qcopy(sib, sib, 0, QP, dev(cc=1 - core), 0).wait_recv()),
+        ("qsib", lambda: qwait(0, QP)),
         ("qf_sib", lambda: qfeat(sib, 0, QP)),
         ("far_sum", far_sum),
         ("qlink3", lambda: qlink(12, QP)),
         ("e3_0", lambda: e3(0)),
-        ("qrelay1", lambda: qrelay(0, 8)),
+        ("qrelay1", lambda: qrelay(0)),
         ("qf_zs", lambda: qfeat(zs, 0, 8)),
         ("e3_1", lambda: e3(1)),
-        ("qtwin1", lambda: qtwin(0, 8)),
+        ("e4a_0", lambda: e4(0, 0)),
+        ("qtwin1", lambda: qwait(3, 8)),
         ("qf_tw", lambda: qfeat(zs2, 0, 8)),
+        ("e4a_1", lambda: e4(1, 0)),
         ("far_back", far_back),
-        ("qrelay2", lambda: qrelay(8, QP)),
+        ("qrelay2", lambda: qrelay(1)),
         ("qf_zs2", lambda: qfeat(zs, 8, QP)),
         ("e3_2", lambda: e3(2)),
         ("twin0", lambda: twin(0)),
-        ("qtwin2", lambda: qtwin(8, QP)),
+        ("qtwin2", lambda: qwait(4, 8)),
         ("qf_tw2", lambda: qfeat(zs2, 8, QP)),
         ("e3_3", lambda: e3(3)),
+        ("e4b_0", lambda: e4(0, 1)),
         ("take3", lambda: take(3)),
+        ("e4a_2", lambda: e4(2, 0)),
         ("take1", lambda: take(1)),
-        ("e4_0", lambda: e4(0)),
+        ("e4b_1", lambda: e4(1, 1)),
         ("twin3", lambda: twin(3)),
         ("twin1", lambda: twin(1)),
         ("take2", lambda: take(2)),
-        ("e4_1", lambda: e4(1)),
+        ("e4a_3", lambda: e4(3, 0)),
         ("twin2", lambda: twin(2)),
         ("mix0", lambda: mix(0, 16)),
-        ("e4_2", lambda: e4(2)),
+        ("e4b_2", lambda: e4(2, 1)),
         ("mix1", lambda: mix(16, 32)),
+        ("e4b_3", lambda: e4(3, 1)),
         ("e5_0", lambda: e5(0)),
-        ("e4_3", lambda: e4(3)),
         ("pr_0", lambda: all_tokens(0)),
         ("e5_1", lambda: e5(1)),
         ("pr_1", lambda: all_tokens(1)),
@@ -486,17 +491,8 @@
             pltpu.VMEM((32, 256, 256), BF),
             pltpu.VMEM((4 * T, D), BF),
             pltpu.VMEM((NC, 4 * T, CW), BF),
-            dma((NC + 3,)),
-            dma, dma((NC, 2, 16)),
-            dma, dma((3, QP)),
-            dma, dma,
-            dma((4,)), dma((4,)),
-            dma((3,)), dma((3,)),
-            dma((3,)), dma((3,)),
-            dma((4,)), dma((4,)),
-            dma((4,)), dma((4,)),
-            dma((NC, 3)), dma((NC, 3)),
-            pltpu.SemaphoreType.REGULAR, pltpu.SemaphoreType.REGULAR,
+            dma((NC + 3,)), dma, dma((NC, 5)), dma, dma((5,)), dma, dma, dma, dma, dma, dma((3,)), dma((4,)), dma, dma,
+            *[pltpu.SemaphoreType.REGULAR] * 4,
         ],
         compiler_params=pltpu.CompilerParams(
             collective_id=0, has_side_effects=True, vmem_limit_bytes=56 * 1024 * 1024

time: 66.4 us -> 63.5 us (0.956)
  Pallas kernels: 65.3 us -> 62.1 us
    pallas_call x1, Pallas kernels: 65.3 us -> 62.1 us  [shards(): pl.pallas_call(kernel, out_shape=pltpu.VMEM((T, D), BF), in_specs=[hbm] *...]
where the time goes in v4:
time: 63.5 us; the launch traced here: 63.1 us
  Pallas kernels  62.1 us (98%)
  local copies, waits for them, and re-layouts  0.97 us (2%)
    pallas_call x1, Pallas kernels, shards(): pl.pallas_call(kernel, out_shape=pltpu.VMEM((T, D), BF), in_specs=[hbm] *...  62.1 us

profile of v4, /device:TPU:1, one launch (start us, length us, event | category | flops | bytes accessed | tf_op | source)
XLA Modules:
  0.0 63.1 jit_solution(7671380653991907075)
XLA Ops:
  0.0 62.1 %attend_project.1 = bf16[128,4096]{1,0:T(8,128)(2,1)S(1)} custom-call(bf16[4096,128]{1,0:T(8,128)(2,1)} %bitcast.11, bf16[4096,128]{1,0:T(8,128)(2,1)} %bitcast.12, bf16[4096,128]{1,0:T(8,128)(2,1)} %bitcast.13, bf16[256,4096]{1,0:T(8,128)(2,1)} %w_hbm.1), custom_call_target="tpu_custom_call" | custom-call | tf_op jit(solution)/shard_map/attend_project/pallas_call | solution.py:471
  62.2 1.0 %copy.6 = bf16[1,128,4096]{2,1,0:T(8,128)(2,1)} copy(bf16[1,128,4096]{2,1,0:T(8,128)(2,1)S(1)} %bitcast.10) | data formatting | bytes 2097152

commit v5 on v4

--- a/solution.py
+++ b/solution.py
@@ -12,6 +12,8 @@
 T = 128
 NC = 4
 CW = 256
+CHUNKS = ((0, 0, 256), (1, 0, 256), (2, 0, 256), (3, 0, 256))
+LEFT = (0, 1, 0, 1)
 SR = 80
 QP = 16
 
@@ -67,7 +69,7 @@
     lk = pltpu.make_async_copy(k_hbm, kbuf, lsem.at[NC])
     lv = pltpu.make_async_copy(v_hbm, vbuf, lsem.at[NC + 1])
     lq = pltpu.make_async_copy(q_hbm, qbuf.at[me], lsem.at[NC + 2])
-    for c in lw + [lk, lv, lq]:
+    for c in lw:
         c.start()
 
     barrier = pltpu.get_barrier_semaphore()
@@ -85,6 +87,9 @@
     def _():
         tell(barrier, twin_core)
 
+    for c in (lk, lv, lq):
+        c.start()
+
     @pl.when(core == 0)
     def _():
         pl.semaphore_wait(barrier, 9)
@@ -116,7 +121,8 @@
         dy, dx = (ds, dp) if h == 0 else (dp, ds)
         ty, tx = (ts, tp) if h == 0 else (tp, ts)
         blk = ((y + dy + 4) % 4) * 4 + (x + dx + 4) % 4
-        ref = wbuf.at[c, pl.ds(pl.multiple_of(blk * 256 + h * 128, 128), 128), :]
+        buf, lo, width = CHUNKS[c]
+        ref = wbuf.at[buf, pl.ds(pl.multiple_of(blk * 256 + h * 128, 128), 128), pl.ds(lo, width)]
         pltpu.make_async_remote_copy(
             src_ref=ref, dst_ref=ref, send_sem=w_ss,
             recv_sem=w_rs.at[c, groups.get(((dp - tp) % 4, (ds - ts) % 4), 4)],
@@ -124,7 +130,8 @@
         ).start()
 
     def wwait(c, g):
-        drain(wbuf.at[c, pl.ds(0, (4, 2, 4, 4, 16)[g] * 128), :], w_rs.at[c, g])
+        buf, lo, width = CHUNKS[c]
+        drain(wbuf.at[buf, pl.ds(0, (4, 2, 4, 4, 16)[g] * 128), pl.ds(lo, width)], w_rs.at[c, g])
 
     def e0(c):
         for h in (0, 1):
@@ -134,7 +141,7 @@
     def e1(c):
         wwait(c, 0)
         for h in (0, 1):
-            wsend(c, h, *(((-1, 0, 1, 0), (1, 0, -1, 0))[c % 2]))
+            wsend(c, h, *(((-1, 0, 1, 0), (1, 0, -1, 0))[LEFT[c]]))
             for dp in (-1, 1):
                 wsend(c, h, dp, 0, 0, 1)
                 wsend(c, h, dp, 0, 0, -1)
@@ -304,18 +311,23 @@
         for n in (2, 3, 0, 1):
             g1copy(n).start()
         gdcopy(0).start()
-        prep(core, cls)
-
-    def take(dk):
+        prep(0, core, cls)
+
+    order = ((core, 0), (1 - core, 0), (core, 3), (core, 1), (1 - core, 3), (1 - core, 1), (core, 2), (1 - core, 2))
+
+    def take(n, dk):
         drain(gat.at[core, cls], g1_rs.at[{3: 0, 1: 1, 2: 2}[dk]])
         gdcopy(dk).start()
-        prep(core, (cls + dk) % 4)
-
-    def twin(dk):
+        prep(n, core, (cls + dk) % 4)
+        mix(n - 1)
+
+    def twin(n, dk, before=True):
         gdcopy(dk).wait_recv()
-        prep(1 - core, (cls + dk) % 4)
-
-    def prep(half, k):
+        prep(n, 1 - core, (cls + dk) % 4)
+        if before:
+            mix(n - 1)
+
+    def prep(step, half, k):
         row = lax.broadcasted_iota(jnp.int32, (16, 256), 0)
         col = lax.broadcasted_iota(jnp.int32, (16, 256), 1) // 128
         pick = jnp.where(row == 8 * col, 1.0 / 64.0, 0.0).astype(BF)
@@ -324,68 +336,81 @@
             s = gat[half, k, m]
             a = s[0:64].astype(F32)
             n = lax.dot_general(s[64:80], pick, (((0,), (0,)), ((), ())), preferred_element_type=F32)
-            pair = 16 * half + 4 * m + k
-            rhs[pair, 0:64, 0:128] = jnp.where(lane, a, 0.0).astype(BF)
-            rhs[pair, 64:128, 0:128] = jnp.where(lane, 0.0, a).astype(BF)
-            rhs[pair, 128:256, 0:128] = zero
-            rhs[pair, 0:64, 128:256] = jnp.where(lane, n[0:64, 0:128], 0.0).astype(BF)
-            rhs[pair, 64:128, 128:256] = jnp.where(lane, 0.0, n[64:128, 0:128]).astype(BF)
-            rhs[pair, 128:192, 128:256] = jnp.where(lane, n[0:64, 128:256], 0.0).astype(BF)
-            rhs[pair, 192:256, 128:256] = jnp.where(lane, 0.0, n[64:128, 128:256]).astype(BF)
-
-    def mix(lo, hi):
-        def body(i, _):
-            for j in range(4):
-                pair = 4 * i + j
-                r = pl.ds(pl.multiple_of(pair * 128, 128), 128)
-                w = rhs[pair]
-                for u in range(4):
-                    t0 = pl.ds(u * T, T)
-                    f = qf[t0, r]
-                    g = jnp.dot(jnp.concatenate([f, f], axis=1), w, preferred_element_type=F32)
-                    mixed[t0, r] = (g[:, 0:128] / (g[:, 128:256] + 1e-3 / 64.0)).astype(BF)
-            return 0
-
-        lax.fori_loop(lo // 4, hi // 4, body, 0)
-
-    others = ((sib, dev(cc=1 - core)), (zs, dev(zz=zback)), (zs2, dev(zz=znext, cc=1 - core)))
+            at = 4 * step + m
+            rhs[at, 0:64, 0:128] = jnp.where(lane, a, 0.0).astype(BF)
+            rhs[at, 64:128, 0:128] = jnp.where(lane, 0.0, a).astype(BF)
+            rhs[at, 128:256, 0:128] = zero
+            rhs[at, 0:64, 128:256] = jnp.where(lane, n[0:64, 0:128], 0.0).astype(BF)
+            rhs[at, 64:128, 128:256] = jnp.where(lane, 0.0, n[64:128, 0:128]).astype(BF)
+            rhs[at, 128:192, 128:256] = jnp.where(lane, n[0:64, 128:256], 0.0).astype(BF)
+            rhs[at, 192:256, 128:256] = jnp.where(lane, 0.0, n[64:128, 128:256]).astype(BF)
+
+    def mix(step):
+        half, dk = order[step]
+        k = (cls + dk) % 4
+        for m in range(4):
+            r = pl.ds(pl.multiple_of((16 * half + 4 * m + k) * 128, 128), 128)
+            w = rhs[4 * step + m]
+            for u in range(4):
+                t0 = pl.ds(u * T, T)
+                f = qf[t0, r]
+                g = jnp.dot(jnp.concatenate([f, f], axis=1), w, preferred_element_type=F32)
+                mixed[t0, r] = (g[:, 0:128] / (g[:, 128:256] + 1e-3 / 64.0)).astype(BF)
 
     def rows(slot):
         return pl.ds(pl.multiple_of(slot * T, T), T)
 
     def cols(c):
-        return pl.ds(pl.multiple_of(quarter * (NC * CW) + c * CW, CW), CW)
-
-    def ocopy(c, n):
-        s, target = others[n]
+        buf, lo, width = CHUNKS[c]
+        return pl.ds(pl.multiple_of(quarter * (NC * CW) + buf * CW + lo, 128), width)
+
+    def ocopy(c, slot, target):
+        buf, lo, width = CHUNKS[c]
         return pltpu.make_async_remote_copy(
-            src_ref=obuf.at[c, rows(s), :], dst_ref=out_ref.at[:, cols(c)],
-            send_sem=o_ss, recv_sem=o_rs,
-            device_id=target, device_id_type=MESH,
-        )
-
-    def part(c, slot):
-        return jnp.dot(mixed[rows(slot), :], wbuf[c], preferred_element_type=F32).astype(BF)
-
-    def far_tokens(c):
-        obuf[c, rows(zs)] = part(c, zs)
-        obuf[c, rows(zs2)] = part(c, zs2)
-        ocopy(c, 1).start()
-        ocopy(c, 2).start()
-
-    def all_tokens(c):
-        far = pl.ds(2 * T, 2 * T)
-        obuf[c, far] = jnp.dot(mixed[far, :], wbuf[c], preferred_element_type=F32).astype(BF)
-        near = pl.ds(0, 2 * T)
-        obuf[c, near] = jnp.dot(mixed[near, :], wbuf[c], preferred_element_type=F32).astype(BF)
-        for n in (1, 2, 0):
-            ocopy(c, n).start()
-        out_ref[:, cols(c)] = obuf[c, rows(me)]
+            src_ref=obuf.at[buf, rows(slot), pl.ds(lo, width)], dst_ref=out_ref.at[:, cols(c)],
+            send_sem=o_ss, recv_sem=o_rs, device_id=target, device_id_type=MESH,
+        )
+
+    znear = {2: dev(zz=(z + 1) % 16, cc=0), 3: dev(zz=(z + 15) % 16, cc=1)}
+
+    def part(c, r, k=pl.ds(0, D)):
+        buf, lo, width = CHUNKS[c]
+        return jnp.dot(mixed[r, k], wbuf[buf, k, lo : lo + width], preferred_element_type=F32)
+
+    def put(c, r, value):
+        buf, lo, width = CHUNKS[c]
+        obuf[buf, r, lo : lo + width] = value.astype(BF)
+
+    def own(c):
+        buf, lo, width = CHUNKS[c]
+        ocopy(c, sib, twin_core).start()
+        out_ref[:, cols(c)] = obuf[buf, rows(me), lo : lo + width]
+
+    def project(c):
+        for first in (2, 0):
+            r = pl.ds(first * T, 2 * T)
+            put(c, r, part(c, r))
+        ocopy(c, 2, znear[2]).start()
+        ocopy(c, 3, znear[3]).start()
+        own(c)
+
+    def far_tokens(c, halves):
+        for slot in (2, 3):
+            r = pl.ds(slot * T, T)
+            if halves:
+                put(c, r, part(c, r, pl.ds(0, D // 2)) + part(c, r, pl.ds(D // 2, D // 2)))
+                ocopy(c, slot, znear[slot]).start()
+            else:
+                put(c, r, part(c, r))
+        if not halves:
+            for slot in (2, 3):
+                ocopy(c, slot, znear[slot]).start()
 
     def near_tokens(c):
-        obuf[c, rows(sib)] = part(c, sib)
-        out_ref[:, cols(c)] = part(c, me)
-        ocopy(c, 0).start()
+        for slot in (0, 1):
+            r = pl.ds(slot * T, T)
+            put(c, r, part(c, r))
+        own(c)
 
     def o_wait():
         drain(obuf.at[pl.ds(0, 3)], o_rs)
@@ -406,9 +431,9 @@
         ("qlink1", lambda: qlink(2, 6)),
         ("e1_0", lambda: e1(0)),
         ("far_ready", far_ready),
+        ("e1_1", lambda: e1(1)),
         ("near_sum", near_sum),
         ("qlink2", lambda: qlink(6, 12)),
-        ("e1_1", lambda: e1(1)),
         ("e1_2", lambda: e1(2)),
         ("qf_me", lambda: qfeat(me, 0, QP)),
         ("e1_3", lambda: e1(3)),
@@ -424,36 +449,37 @@
         ("qtwin1", lambda: qwait(3, 8)),
         ("qf_tw", lambda: qfeat(zs2, 0, 8)),
         ("e4a_1", lambda: e4(1, 0)),
+        ("e3_2", lambda: e3(2)),
         ("far_back", far_back),
         ("qrelay2", lambda: qrelay(1)),
         ("qf_zs2", lambda: qfeat(zs, 8, QP)),
-        ("e3_2", lambda: e3(2)),
-        ("twin0", lambda: twin(0)),
+        ("twin0", lambda: twin(1, 0, before=False)),
+        ("e4b_0", lambda: e4(0, 1)),
         ("qtwin2", lambda: qwait(4, 8)),
+        ("e3_3", lambda: e3(3)),
         ("qf_tw2", lambda: qfeat(zs2, 8, QP)),
-        ("e3_3", lambda: e3(3)),
-        ("e4b_0", lambda: e4(0, 1)),
-        ("take3", lambda: take(3)),
+        ("e4b_1", lambda: e4(1, 1)),
+        ("mix0", lambda: mix(0)),
         ("e4a_2", lambda: e4(2, 0)),
-        ("take1", lambda: take(1)),
-        ("e4b_1", lambda: e4(1, 1)),
-        ("twin3", lambda: twin(3)),
-        ("twin1", lambda: twin(1)),
-        ("take2", lambda: take(2)),
+        ("take3", lambda: take(2, 3)),
+        ("take1", lambda: take(3, 1)),
         ("e4a_3", lambda: e4(3, 0)),
-        ("twin2", lambda: twin(2)),
-        ("mix0", lambda: mix(0, 16)),
+        ("twin3", lambda: twin(4, 3)),
         ("e4b_2", lambda: e4(2, 1)),
-        ("mix1", lambda: mix(16, 32)),
+        ("twin1", lambda: twin(5, 1)),
+        ("take2", lambda: take(6, 2)),
+        ("twin2", lambda: twin(7, 2)),
         ("e4b_3", lambda: e4(3, 1)),
+        ("mix7", lambda: mix(7)),
         ("e5_0", lambda: e5(0)),
-        ("pr_0", lambda: all_tokens(0)),
+        ("pr_0", lambda: project(0)),
         ("e5_1", lambda: e5(1)),
-        ("pr_1", lambda: all_tokens(1)),
+        ("pr_1", lambda: project(1)),
         ("e5_2", lambda: e5(2)),
-        ("pr_2", lambda: all_tokens(2)),
+        ("prf_2", lambda: far_tokens(2, False)),
         ("e5_3", lambda: e5(3)),
-        ("prf_3", lambda: far_tokens(3)),
+        ("prf_3", lambda: far_tokens(3, True)),
+        ("prn_2", lambda: near_tokens(2)),
         ("prn_3", lambda: near_tokens(3)),
         ("o_wait", o_wait),
         ("finish", finish),

time: 63.5 us -> 63 us (level)
  the two profiles are of different devices: /device:TPU:1 before, /device:TPU:2 now
where the time goes in v5:
time: 63 us; the launch traced here: 62.9 us
  Pallas kernels  61.9 us (98%)
  local copies, waits for them, and re-layouts  0.97 us (2%)
    pallas_call x1, Pallas kernels, shards(): pl.pallas_call(kernel, out_shape=pltpu.VMEM((T, D), BF), in_specs=[hbm] *...  61.9 us

profile of v5, /device:TPU:2, one launch (start us, length us, event | category | flops | bytes accessed | tf_op | source)
XLA Modules:
  0.0 62.9 jit_solution(3734220197515718258)
XLA Ops:
  0.0 61.9 %attend_project.1 = bf16[128,4096]{1,0:T(8,128)(2,1)S(1)} custom-call(bf16[4096,128]{1,0:T(8,128)(2,1)} %bitcast.11, bf16[4096,128]{1,0:T(8,128)(2,1)} %bitcast.12, bf16[4096,128]{1,0:T(8,128)(2,1)} %bitcast.13, bf16[256,4096]{1,0:T(8,128)(2,1)} %w_hbm.1), custom_call_target="tpu_custom_call" | custom-call | tf_op jit(solution)/shard_map/attend_project/pallas_call | solution.py:497
  61.9 1.0 %copy.6 = bf16[1,128,4096]{2,1,0:T(8,128)(2,1)} copy(bf16[1,128,4096]{2,1,0:T(8,128)(2,1)S(1)} %bitcast.10) | data formatting | bytes 2097152

commit v6 on v5

--- a/solution.py
+++ b/solution.py
@@ -115,7 +115,7 @@
     def drain(ref, sem):
         pltpu.make_async_copy(ref, ref, sem).wait()
 
-    groups = {(1, 0): 0, (3, 0): 0, (2, 0): 1, (0, 3): 2, (3, 1): 2, (1, 3): 3, (2, 1): 3}
+    groups = {(1, 0): 0, (3, 0): 0, (2, 0): 1, (0, 3): 2, (3, 1): 2, (1, 3): 2, (2, 1): 3}
 
     def wsend(c, h, dp, ds, tp, ts):
         dy, dx = (ds, dp) if h == 0 else (dp, ds)
@@ -131,7 +131,7 @@
 
     def wwait(c, g):
         buf, lo, width = CHUNKS[c]
-        drain(wbuf.at[buf, pl.ds(0, (4, 2, 4, 4, 16)[g] * 128), pl.ds(lo, width)], w_rs.at[c, g])
+        drain(wbuf.at[buf, pl.ds(0, (4, 2, 6, 2, 16)[g] * 128), pl.ds(lo, width)], w_rs.at[c, g])
 
     def e0(c):
         for h in (0, 1):
@@ -155,7 +155,7 @@
     def e4(c, late):
         wwait(c, 2 + late)
         for h in (0, 1):
-            for dp, ds in (((0, -1), (-1, 1)), ((1, -1), (2, 1)))[late]:
+            for dp, ds in (((0, -1), (-1, 1), (1, -1)), ((2, 1),))[late]:
                 wsend(c, h, dp, ds, 0, -ds)
 
     def e5(c):

time: 63 us -> 63 us (level)
  no operation moved by 1% of the time
where the time goes in v6:
time: 63 us; the launch traced here: 62.9 us
  Pallas kernels  61.9 us (98%)
  local copies, waits for them, and re-layouts  0.97 us (2%)
    pallas_call x1, Pallas kernels, shards(): pl.pallas_call(kernel, out_shape=pltpu.VMEM((T, D), BF), in_specs=[hbm] *...  61.9 us

profile of v6, /device:TPU:2, one launch (start us, length us, event | category | flops | bytes accessed | tf_op | source)
XLA Modules:
  0.0 62.9 jit_solution(7939729807046411104)
XLA Ops:
  0.0 61.9 %attend_project.1 = bf16[128,4096]{1,0:T(8,128)(2,1)S(1)} custom-call(bf16[4096,128]{1,0:T(8,128)(2,1)} %bitcast.11, bf16[4096,128]{1,0:T(8,128)(2,1)} %bitcast.12, bf16[4096,128]{1,0:T(8,128)(2,1)} %bitcast.13, bf16[256,4096]{1,0:T(8,128)(2,1)} %w_hbm.1), custom_call_target="tpu_custom_call" | custom-call | tf_op jit(solution)/shard_map/attend_project/pallas_call | solution.py:497
  61.9 1.0 %copy.6 = bf16[1,128,4096]{2,1,0:T(8,128)(2,1)} copy(bf16[1,128,4096]{2,1,0:T(8,128)(2,1)S(1)} %bitcast.10) | data formatting | bytes 2097152
